TPU v7x, 32 devices: a whole 2x2x4 slice. The times are simulated.
32 devices in a mesh: seq: 16 (over z, y, x), head: 2 (over core).
Axes of the slice: x: 2, y: 2, z: 4, core: 2. Of those that a mesh axis runs over, the one named last changes fastest.
Arguments:
- tokens: bfloat16 [8192, 3584], P('seq', 'head'), may hold values from -6 to 6
- pre_gain: float32 [3584], replicated, may hold values from 0.5 to 1.5
- query_weight: bfloat16 [3584, 2048], P(None, 'head'), may hold values from -0.375 to 0.375
- key_weight: bfloat16 [3584, 1024], P(None, 'head'), may hold values from -0.375 to 0.375
- value_weight: bfloat16 [3584, 1024], P(None, 'head'), may hold values from -0.09375 to 0.09375
- out_weight: bfloat16 [2048, 3584], P('head'), may hold values from -0.5 to 0.5
- post_gain: float32 [3584], P('head'), may hold values from 0.5 to 1.5
Outputs:
- layer_out: bfloat16 [8192, 3584], P('seq', 'head')
All inputs are finite; a program needn't handle non-finite values.
Results may differ from a plain program's by a relative error of at most 0.013.
The roundings to bfloat16 on the way count: a program that leaves them out, or rounds other values in their place, can miss the bound.
Values may be sent and summed in bfloat16 or wider, within the bound.
No kernel may reach another device: no remote copies, remote signals or barrier semaphores. Data moves between devices by JAX's collectives and lax.ppermute only.
A program may use at most 192 MiB of HBM per device.

v0:
```python
import functools

import jax
import jax.numpy as jnp
from jax import lax
from jax.experimental import pallas as pl
from jax.experimental.pallas import tpu as pltpu
from jax.sharding import PartitionSpec as P


HD = 256
WINDOW = 4096

softcap_limit = 50.0
rope_base = 10000.0
norm_epsilon = 1e-06


LOG2E = 1.4426950408889634
ROW_CHUNK = 256


def rope_tables(positions, head_dim):
    midpoint = head_dim // 2
    frequency = jnp.exp(
        -jnp.log(rope_base) * (2.0 * jnp.arange(midpoint, dtype=jnp.float32) / head_dim)
    )
    angles = positions.astype(jnp.float32)[:, None] * frequency[None, :]
    return jnp.cos(angles), jnp.sin(angles)


def dot(left, right):
    return jnp.dot(left, right, preferred_element_type=jnp.float32)


VMEM = pl.BlockSpec(memory_space=pltpu.VMEM)
SMEM = pl.BlockSpec(memory_space=pltpu.SMEM)
FAR = pl.BlockSpec(memory_space=pltpu.HBM)
MIB = 1024 * 1024
GRANT = 8
SLOW = 10**11


class Fetch:
    def __init__(self, arrays, outputs):
        self.arrays = arrays
        self.outputs = outputs
        self.plan = [(k, *block) for k, (_, blocks) in enumerate(outputs) for block in blocks]

    def shapes(self):
        return [jax.ShapeDtypeStruct(shape, jnp.bfloat16) for shape, _ in self.outputs]

    def scratch(self):
        return [pltpu.SemaphoreType.DMA((len(self.plan),))] if self.plan else []

    def start(self, numbers, arrays, outputs, arrived):
        copies = []
        for k, (index, array, row, column, shape, *starts) in enumerate(self.plan):
            source = []
            for start, size in zip(starts, shape):
                first = start or 0
                if callable(first):
                    first = pl.multiple_of(first(numbers), size)
                source.append(pl.ds(first, size))
            copy = pltpu.make_async_copy(
                arrays[array].at[source[0], source[1]],
                outputs[index].at[pl.ds(row, shape[0]), pl.ds(column, shape[1])],
                arrived.at[k],
            )
            copy.start()
            copies.append(copy)
        return copies


def kernel_call(body, fetch, numbers, operands, out_shape, scratch, grant, flops, aliases=None):
    n_operands, n_arrays = len(operands), len(fetch.arrays)
    n_out, n_fetched = len(out_shape), len(fetch.outputs)

    def kernel(numbers_ref, *refs):
        refs = list(refs)
        inputs, refs = refs[:n_operands], refs[n_operands:]
        arrays, refs = refs[:n_arrays], refs[n_arrays:]
        outputs, refs = refs[:n_out], refs[n_out:]
        fetched, refs = refs[:n_fetched], refs[n_fetched:]
        copies = []
        if fetch.plan:
            copies = fetch.start(numbers_ref, arrays, fetched, refs[-1])
            refs = refs[:-1]
        body(numbers_ref, inputs, outputs, refs)
        for copy in copies:
            copy.wait()

    moved = sum(x.size * x.dtype.itemsize for x in (*operands, *out_shape))
    return pl.pallas_call(
        kernel,
        out_shape=list(out_shape) + fetch.shapes(),
        in_specs=[SMEM] + [VMEM] * n_operands + [FAR] * n_arrays,
        out_specs=[VMEM] * (n_out + n_fetched),
        scratch_shapes=list(scratch) + fetch.scratch(),
        input_output_aliases={1 + i: o for i, o in (aliases or {}).items()},
        compiler_params=pltpu.CompilerParams(vmem_limit_bytes=grant * MIB),
        cost_estimate=pl.CostEstimate(flops=flops, bytes_accessed=moved, transcendentals=0),
    )(numbers, *operands, *fetch.arrays)


NOTHING = Fetch([], [])


def lane_sums(value, lanes):
    part = value[:, :lanes]
    for k in range(lanes, value.shape[1], lanes):
        part = part + value[:, k : k + lanes]
    return part


def sum_squares(numbers, tokens, ready, fetch):
    rows, part = tokens.shape
    lanes = min(128, part)

    def body(scalars, inputs, outputs, scratch):
        step = min(16, rows)

        def some_rows(t, carry):
            at = pl.ds(pl.multiple_of(t * step, step), step)
            total = None
            for k in range(0, part, lanes):
                value = inputs[0][at, k : k + lanes].astype(jnp.float32)
                value = value * value
                total = value if total is None else total + value
            outputs[0][at, :] = total
            return carry

        lax.fori_loop(0, rows // step, some_rows, 0, unroll=2)

    out = [jax.ShapeDtypeStruct((rows, lanes), jnp.float32)]
    return kernel_call(body, fetch, numbers, [tokens, *ready], out, [], 6, SLOW)


def write_blocks(numbers, normed, firsts, weight_refs, blocks, tables, out_ref):
    cosine, sine_part = tables
    column = 0
    for weight, width, first, turned in blocks:
        here = pl.ds(pl.multiple_of(first(numbers), width), width)
        product = None
        part = normed.shape[1] // len(firsts)
        for k, start in enumerate(firsts):
            deep = pl.ds(pl.multiple_of(start(numbers), part), part)
            term = dot(normed[:, k * part : (k + 1) * part], weight_refs[weight][deep, here])
            product = term if product is None else product + term
        for head in range(0, width, HD):
            middle, end = head + HD // 2, head + HD
            leading, trailing = product[:, head:middle], product[:, middle:end]
            if turned:
                cos, sin = cosine[...], sine_part[...]
                leading, trailing = leading * cos - trailing * sin, trailing * cos + leading * sin
            out_ref[:, column + head : column + middle] = leading.astype(jnp.bfloat16)
            out_ref[:, column + middle : column + end] = trailing.astype(jnp.bfloat16)
        column += width


def normed_projection(
    numbers, shards, firsts, gain, squares, tables, weights, blocks, fetch
):
    n = len(shards)
    rows, part = shards[0].shape

    def body(scalars, inputs, outputs, scratch):
        shard_refs, square_refs = inputs[:n], inputs[n : 2 * n]
        gain_ref, cosine, sine_part = inputs[2 * n : 2 * n + 3]
        weight_refs = inputs[2 * n + 3 :]
        normed, out_ref = outputs
        scale_ref = scratch[0]
        total = square_refs[0][...]
        for ref in square_refs[1:]:
            total = total + ref[...]
        total = jnp.sum(total, axis=-1, keepdims=True)
        scale = lax.rsqrt(total / (part * n) + norm_epsilon)
        scale_ref[...] = jnp.broadcast_to(scale, scale_ref.shape)
        gains = scratch[1]
        step = gains.shape[0]
        lanes = scale_ref.shape[1]
        for k in range(n):
            first = firsts[k](scalars)
            for column in range(0, part, lanes):
                gain = gain_ref[pl.ds((first + column) // lanes, 1), :]
                here = slice(k * part + column, k * part + column + lanes)
                gains[:, here] = jnp.broadcast_to(gain, (step, lanes))

        def norm_rows(t, carry):
            at = pl.ds(pl.multiple_of(t * step, step), step)
            scale = scale_ref[at, :]
            for k, shard in enumerate(shard_refs):
                for column in range(0, part, lanes):
                    here = slice(k * part + column, k * part + column + lanes)
                    value = shard[at, column : column + lanes].astype(jnp.float32)
                    value = value * scale * gains[:, here]
                    normed[at, here] = value.astype(jnp.bfloat16)
            return carry

        lax.fori_loop(0, rows // step, norm_rows, 0, unroll=2)
        write_blocks(scalars, normed, firsts, weight_refs, blocks, (cosine, sine_part), out_ref)

    width = sum(width for _, width, _, _ in blocks)
    out = [
        jax.ShapeDtypeStruct((rows, part * n), jnp.bfloat16),
        jax.ShapeDtypeStruct((rows, width), jnp.bfloat16),
    ]
    operands = [*shards, *squares, gain, *tables, *weights]
    flops = 2 * rows * part * n * width
    scratch = [
        pltpu.VMEM((rows, min(128, part)), jnp.float32),
        pltpu.VMEM((min(16, rows), part * n), jnp.float32),
    ]
    return kernel_call(body, fetch, numbers, operands, out, scratch, GRANT, flops)


def projection(numbers, normed, firsts, tables, weights, outputs, fetch):
    rows = normed.shape[0]

    def body(scalars, inputs, outs, scratch):
        for blocks, out_ref in zip(outputs, outs):
            write_blocks(
                scalars, inputs[0], firsts, inputs[3:], blocks, inputs[1:3], out_ref
            )

    widths = [sum(width for _, width, _, _ in blocks) for blocks in outputs]
    out = [jax.ShapeDtypeStruct((rows, width), jnp.bfloat16) for width in widths]
    flops = 2 * normed.size * sum(widths)
    return kernel_call(body, fetch, numbers, [normed, *tables, *weights], out, [], 8, flops)


def out_projection(numbers, lefts, weight, total, last):
    n = len(lefts)
    rows, width = lefts[0].shape
    out_width = weight.shape[1]
    lanes = min(128, out_width)
    columns = 256 if out_width % 256 == 0 else out_width

    def body(scalars, inputs, outputs, scratch):
        weight_ref = inputs[n]
        left = scratch[0]
        for k in range(n):
            left[:, k * width : (k + 1) * width] = inputs[k][...]
        for column in range(0, out_width, columns):
            here = slice(column, column + columns)
            value = dot(left[...], weight_ref[:, here])
            if total is not None:
                value = value + inputs[n + 1][:, here]
            outputs[0][:, here] = value
            if last:
                part = lane_sums(value * value, lanes)
                if column == 0:
                    outputs[1][...] = part
                else:
                    outputs[1][...] = outputs[1][...] + part

    out = [jax.ShapeDtypeStruct((rows, out_width), jnp.float32)]
    if last:
        out.append(jax.ShapeDtypeStruct((rows, lanes), jnp.float32))
    operands = [*lefts, weight] + ([] if total is None else [total])
    aliases = {} if total is None else {n + 1: 0}
    scratch = [pltpu.VMEM((rows, n * width), jnp.bfloat16)]
    flops = 2 * rows * n * width * out_width
    return kernel_call(body, NOTHING, numbers, operands, out, scratch, 8, flops, aliases)


def finish_kernel(n, tokens, share, gain, *refs):
    square_refs, out, scale_ref = refs[:n], refs[n], refs[n + 1]
    block, part = out.shape
    lanes = scale_ref.shape[1]
    base = pl.program_id(0) * block
    at = pl.ds(pl.multiple_of(base, block), block)
    total = square_refs[0][at, :]
    for ref in square_refs[1:]:
        total = total + ref[at, :]
    total = jnp.sum(total, axis=-1, keepdims=True)
    scale = lax.rsqrt(total / (part * n) + norm_epsilon)
    scale_ref[...] = jnp.broadcast_to(scale, scale_ref.shape)
    step = min(16, block)

    def some_rows(t, carry):
        here = pl.ds(pl.multiple_of(t * step, step), step)
        at = pl.ds(pl.multiple_of(base + t * step, step), step)
        scale = scale_ref[here, :]
        for column in range(0, part, lanes):
            columns = slice(column, column + lanes)
            value = gain[column // lanes : column // lanes + 1, :] * share[at, columns] * scale
            value = tokens[at, columns].astype(jnp.float32) + value
            out[here, columns] = value.astype(jnp.bfloat16)
        return carry

    lax.fori_loop(0, block // step, some_rows, 0, unroll=2)


def finish(tokens, share, gain, squares):
    rows, part = tokens.shape
    step = min(128, rows)
    return pl.pallas_call(
        functools.partial(finish_kernel, len(squares)),
        grid=(rows // step,),
        out_shape=jax.ShapeDtypeStruct((rows, part), jnp.bfloat16),
        in_specs=[VMEM] * (3 + len(squares)),
        out_specs=pl.BlockSpec((step, part), lambda t: (t, 0)),
        scratch_shapes=[pltpu.VMEM((step, min(128, part)), jnp.float32)],
        compiler_params=pltpu.CompilerParams(vmem_limit_bytes=8 * MIB),
        cost_estimate=pl.CostEstimate(
            flops=8 * rows * part, bytes_accessed=8 * rows * part, transcendentals=0
        ),
    )(tokens, share, gain, *squares)


def attend(numbers, query_blocks, key_blocks, queries, pieces, totals, last, full, fetch):
    n_q, n_kv = len(queries), len(pieces)
    rows, width = queries[0].shape
    heads = width // HD
    lanes = min(128, rows)
    window_blocks = WINDOW // rows
    first = totals is None
    acc_shape = (n_q, rows, width)
    den_shape = (n_q, rows, heads * lanes)
    chunk = min(ROW_CHUNK, rows)

    def body(scalars, inputs, outputs, scratch):
        q_refs, kv_refs = inputs[:n_q], inputs[n_q : n_q + n_kv]
        kv_all, key_numbers = scratch[:2]
        acc, den = scratch[2:] if last else outputs
        for k in range(n_kv):
            kv_all[k * rows : (k + 1) * rows, :] = kv_refs[k][...]
            key_numbers[k] = key_blocks[k](scalars)
        if first:
            acc[...] = jnp.zeros_like(acc)
            den[...] = jnp.zeros_like(den)
        elif last:
            acc[...] = inputs[n_q + n_kv][...]
            den[...] = inputs[n_q + n_kv + 1][...]

        def add(r, keys_at, delta):
            for head in range(heads):
                for start in range(0, rows, chunk):
                    at = slice(start, start + chunk)
                    columns = slice(head * HD, (head + 1) * HD)
                    scores = lax.dot_general(
                        q_refs[r][at, columns],
                        kv_all[keys_at, :HD],
                        (((1,), (1,)), ((), ())),
                        preferred_element_type=jnp.float32,
                    )
                    weights = jnp.exp2(
                        jnp.tanh(scores * (HD ** (-0.5) / softcap_limit))
                        * (softcap_limit * LOG2E)
                    )
                    if delta is not None:
                        offset = (
                            lax.broadcasted_iota(jnp.int32, weights.shape, 0)
                            - lax.broadcasted_iota(jnp.int32, weights.shape, 1)
                            + (delta * rows + start)
                        )
                        allowed = (offset >= 0) & (offset < window_blocks * rows)
                        weights = jnp.where(allowed, weights, 0.0)
                    lane_at = slice(head * lanes, (head + 1) * lanes)
                    den[r, at, lane_at] = den[r, at, lane_at] + lane_sums(weights, lanes)
                    acc[r, at, columns] = acc[r, at, columns] + dot(
                        weights.astype(jnp.bfloat16), kv_all[keys_at, HD:]
                    )

        if full:

            @pl.when(key_numbers[0] >= 0)
            def _():
                for r in range(n_q):
                    add(r, slice(0, n_kv * rows), None)

        else:

            def step(n, carry):
                key_block = key_numbers[n]
                live = key_block >= 0
                deltas = [block(scalars) - key_block for block in query_blocks]
                inside = [(delta > 0) & (delta < window_blocks) for delta in deltas]
                every = functools.reduce(jnp.logical_and, inside)
                keys_at = pl.ds(pl.multiple_of(n * rows, rows), rows)

                @pl.when(live & every)
                def _():
                    for r in range(n_q):
                        add(r, keys_at, None)

                for r in range(n_q):
                    some = (deltas[r] >= 0) & (deltas[r] <= window_blocks)

                    @pl.when(live & some & jnp.logical_not(every))
                    def _():
                        add(r, keys_at, deltas[r])

                return carry

            lax.fori_loop(0, n_kv, step, 0)
        if last:
            for r in range(n_q):
                for head in range(heads):
                    total = jnp.sum(
                        den[r, :, head * lanes : (head + 1) * lanes], axis=-1, keepdims=True
                    )
                    columns = slice(head * HD, (head + 1) * HD)
                    outputs[r][:, columns] = (acc[r, :, columns] / total).astype(jnp.bfloat16)

    scratch = [
        pltpu.VMEM((n_kv * rows, pieces[0].shape[1]), jnp.bfloat16),
        pltpu.SMEM((n_kv,), jnp.int32),
    ]
    operands = [*queries, *pieces] + ([] if first else list(totals))
    aliases = {}
    if last:
        out = [jax.ShapeDtypeStruct((rows, width), jnp.bfloat16)] * n_q
        scratch += [pltpu.VMEM(acc_shape, jnp.float32), pltpu.VMEM(den_shape, jnp.float32)]
    else:
        out = [
            jax.ShapeDtypeStruct(acc_shape, jnp.float32),
            jax.ShapeDtypeStruct(den_shape, jnp.float32),
        ]
        if not first:
            aliases = {n_q + n_kv: 0, n_q + n_kv + 1: 1}
    flops = n_q * n_kv * heads * 4 * rows * rows * HD * 2 // 3
    return kernel_call(body, fetch, numbers, operands, out, scratch, 14, flops, aliases)


def local(tokens, pre_gain, query_weight, key_weight, value_weight, out_weight, post_gain):
    n_seq = lax.axis_size("seq")
    cores = lax.axis_size("head")
    rows, part = tokens.shape
    kv_heads = key_weight.shape[1] // HD
    query_heads = query_weight.shape[1] // HD
    piece_width = query_heads // kv_heads * HD
    plane = cores * kv_heads
    hops = WINDOW // (rows * plane)
    seq = lax.axis_index("seq")
    core = lax.axis_index("head")
    place = seq % plane
    column = place % kv_heads
    row = place // kv_heads

    def over_cores(value, by=1):
        return lax.ppermute(value, "head", [(c, (c + by) % cores) for c in range(cores)])

    def next_plane(value):
        return lax.ppermute(value, "seq", [(i, i + plane) for i in range(n_seq - plane)])

    def route(turn):
        pairs = []
        for s in range(n_seq):
            base, at = s - s % plane, s % plane
            y, x = at // kv_heads, at % kv_heads
            for c in range(cores):
                target = base + c * kv_heads + (x + c + turn) % kv_heads
                pairs.append((s * cores + c, target * cores + y))
        return pairs

    def spread(value, turn):
        return lax.ppermute(value, ("seq", "head"), route(turn))

    def gather_back(value, turn):
        return lax.ppermute(value, ("seq", "head"), [(b, a) for a, b in route(turn)])

    turns = range(kv_heads)
    others = range(1, cores)
    numbers = jnp.stack([core, column, row, seq - place]).astype(jnp.int32)

    def held_by(by, turn, scale):
        def start(ref):
            return lax.rem(ref[1] + lax.rem(ref[0] + cores - by, cores) + turn, kv_heads) * scale

        return start

    shards = [tokens] + [over_cores(tokens, by) for by in others]
    firsts = [
        (lambda ref, by=by: lax.rem(ref[0] + cores - by, cores) * part) for by in range(cores)
    ]
    positions = seq * rows + jnp.arange(rows, dtype=jnp.int32)
    tables = rope_tables(positions, HD)
    lanes = min(128, part)
    gain_in, gain_out = pre_gain.reshape(-1, lanes), post_gain.reshape(-1, lanes)
    (own_squares,) = sum_squares(numbers, tokens, [*tables, gain_in, gain_out], NOTHING)
    kv_weights = [key_weight, value_weight]
    squares = [own_squares] + [over_cores(own_squares, by) for by in others]
    kv_blocks = [
        [(n, HD, held_by(0, turn, HD), n == 0) for n in range(len(kv_weights))] for turn in turns
    ]
    q_blocks = [[(0, piece_width, held_by(0, turn, piece_width), True)] for turn in turns]
    normed, piece = normed_projection(
        numbers,
        shards,
        firsts,
        gain_in,
        squares,
        tables,
        kv_weights,
        kv_blocks[0],
        NOTHING,
    )
    sent = [piece]
    row_blocks = [out_weight]
    out_rows = out_weight.shape[0]
    for turn in turns[1:]:
        fetch = NOTHING
        if turn == 1:
            shape = (out_rows, part)
            columns = [
                (lambda ref, by=by: lax.rem(ref[0] + by, cores) * part) for by in others
            ]
            fetch = Fetch(
                [out_weight], [(shape, [(0, 0, 0, shape, None, first)]) for first in columns]
            )
        piece, *blocks = projection(
            numbers, normed, firsts, tables, kv_weights, [kv_blocks[turn]], fetch
        )
        sent.append(piece)
        row_blocks += [over_cores(block, by) for by, block in zip(others, blocks)]
    q_out = []
    for turn in turns:
        q_out += projection(
            numbers, normed, firsts, tables, [query_weight], [q_blocks[turn]], NOTHING
        )

    travelling = [next_plane(piece) for piece in sent]
    q_pieces = [spread(piece, turn) for turn, piece in enumerate(q_out)]
    levels = [[spread(piece, turn) for turn, piece in enumerate(sent)]]
    level = [spread(piece, turn) for turn, piece in enumerate(travelling)]
    levels.append(level)
    for _ in range(2, hops + 1):
        level = [next_plane(piece) for piece in level]
        levels.append(level)

    def block_of(by, turn, lag):
        def block(ref):
            column_of = lax.rem(ref[1] - ref[2] - turn + cores * plane * kv_heads, kv_heads)
            row_of = lax.rem(ref[0] + cores - by, cores)
            return ref[3] - lag * plane + row_of * kv_heads + column_of

        return block

    query_blocks = [block_of(0, turn, 0) for turn in turns]

    def piece_of(lag, turn, by):
        piece = levels[lag][turn]
        return over_cores(piece, by) if by else piece

    out_fetch = []
    for turn in turns:
        blocks = []
        for by in range(cores):
            blocks.append(
                (
                    by,
                    by * piece_width,
                    0,
                    (piece_width, part),
                    held_by(by, turn, piece_width),
                    None if by else (lambda ref: ref[0] * part),
                )
            )
        out_fetch.append(((piece_width * cores, part), blocks))
    calls = []
    for lag in range(1, hops + 1):
        for turn in turns:
            calls.append([(lag, turn, by) for by in range(cores)])
        if lag == 1:
            calls += [[(0, turn, by) for by in range(cores)] for turn in turns]
    calls[-1:] = [calls[-1][:1], calls[-1][1:]]
    totals = None
    for index, call in enumerate(calls):
        blocks = [block_of(by, turn, lag) for lag, turn, by in call]
        pieces = [piece_of(*key) for key in call]
        last = index == len(calls) - 1
        full = all(0 < lag < hops for lag, _, _ in call)
        fetch = Fetch(row_blocks, out_fetch) if index == len(calls) - 3 else NOTHING
        totals = attend(numbers, query_blocks, blocks, q_pieces, pieces, totals, last, full, fetch)
        if fetch is not NOTHING:
            totals, out_blocks = totals[:2], totals[2:]
    attended = totals
    total = None
    for turn, o in enumerate(attended):
        own = gather_back(o, turn)
        lefts = [own] + [over_cores(own, by) for by in others]
        out = out_projection(numbers, lefts, out_blocks[turn], total, turn == kv_heads - 1)
        total = out[0]
    share, own_squares = out
    squares = [own_squares] + [over_cores(own_squares, by) for by in others]
    return finish(tokens, share, gain_out, squares)


def solution(mesh):
    placed = (
        P("seq", "head"),
        P(),
        P(None, "head"),
        P(None, "head"),
        P(None, "head"),
        P("head", None),
        P("head"),
    )
    return jax.shard_map(
        local, mesh=mesh, in_specs=placed, out_specs=P("seq", "head"), check_vma=False
    )
```

profile of v0, /device:TPU:17, one launch (start us, length us, event | category | flops | bytes accessed | tf_op | source)
XLA Modules:
  0.0 132.7 jit_solution(13559584394246346845)
XLA Ops:
  0.0 0.7 collective-permute-start
  0.7 1.0 multiply_sine_fusion
  1.7 0.1 pad_add_fusion.numbers_ref
  1.8 1.6 %copy-done.2 = bf16[512,1792]{1,0:T(8,128)(2,1)S(1)} copy-done((bf16[512,1792]{1,0:T(8,128)(2,1)S(1)}, bf16[512,1792]{1,0:T(8,128)(2,1)}, u32[]{:S(2)}) %copy-start.2) | copy-done | bytes 1835032
  3.4 0.9 copy-done.4
  4.3 0.7 copy-done.5
  5.0 1.0 shard_map.73.refs_2_
  6.0 0.1 collective-permute-start.1
  6.1 1.5 %collective-permute-done.1.refs_3_ = f32[512,128]{1,0:T(8,128)S(1)} collective-permute-done((f32[512,128]{1,0:T(8,128)S(1)}, f32[512,128]{1,0:T(8,128)S(1)}, u32[]{:S(2)}, u32[]{:S(2)}) %collective-permute-start.1) | collective-permute-done | bytes 262176 | tf_op jit(solution)/shard_map/ppermute | solution.py:443
  7.6 0.0 collective-permute-done.refs_1_
  7.7 0.5 copy-done.1
  8.2 0.5 copy-done.3
  8.7 4.0 %shard_map.74 = (bf16[512,3584]{1,0:T(8,128)(2,1)S(1)}, bf16[512,512]{1,0:T(8,128)(2,1)S(1)}) custom-call(s32[4]{0:T(128)S(1)} %pad_add_fusion.numbers_ref, bf16[512,1792]{1,0:T(8,128)(2,1)S(1)} %copy-done.3, bf16[512,1792]{1,0:T(8,128)(2,1)S(1)} %collective-permute-done.refs_1_, f32[512,128]{1,0:T(8,128)S(1)} %shard_map.73.refs_2_, ...), custom_call_target="tpu_custom_call" | custom-call | flops 1879048192 | bytes 16267264 | tf_op jit(solution)/shard_map/pallas_call | solution.py:94
  12.7 0.0 slice-start.2
  12.7 0.0 slice-start.3
  12.8 2.9 %shard_map.77 = (bf16[512,512]{1,0:T(8,128)(2,1)S(1)}, bf16[1024,1792]{1,0:T(8,128)(2,1)S(1)}) custom-call(s32[4]{0:T(128)S(1)} %pad_add_fusion.numbers_ref, bf16[512,3584]{1,0:T(8,128)(2,1)S(1)} %get-tuple-element.27.refs_0_, f32[512,128]{1,0:T(8,128)S(1)} %get-tuple-element.50.refs_1_.refs_5_, f32[512,128]{1,0:T(8,128)S(1)} %get-tuple-element.49.refs_2_.refs_6_, ...), custom_call_target="tpu_custom_call" | custom-call | flops 1879048192 | bytes 12058624 | tf_op jit(solution)/shard_map/pallas_call | solution.py:94
  15.6 0.1 collective-permute-start.18
  15.7 3.2 %collective-permute-start.8 = (bf16[512,512]{1,0:T(8,128)(2,1)S(1)}, bf16[512,512]{1,0:T(8,128)(2,1)S(1)}, u32[]{:S(2)}, u32[]{:S(2)}) collective-permute-start(bf16[512,512]{1,0:T(8,128)(2,1)S(1)} %get-tuple-element.29), channel_id=1, source_target_pairs={{0,8},{2,10},{4,12},{6,14},{8,16},{10,18},{12,20},{14,22},{16,24},... | collective-permute-start | bytes 1572872 | tf_op jit(solution)/shard_map/ppermute | solution.py:446
  18.9 1.9 %collective-permute-start.4 = (bf16[512,512]{1,0:T(8,128)(2,1)S(1)}, bf16[512,512]{1,0:T(8,128)(2,1)S(1)}, u32[]{:S(2)}, u32[]{:S(2)}) collective-permute-start(bf16[512,512]{1,0:T(8,128)(2,1)S(1)} %get-tuple-element.28), channel_id=1, source_target_pairs={{0,8},{2,10},{4,12},{6,14},{8,16},{10,18},{12,20},{14,22},{16,24},... | collective-permute-start | bytes 1572872 | tf_op jit(solution)/shard_map/ppermute | solution.py:446
  20.9 2.6 %shard_map.76 = bf16[512,512]{1,0:T(8,128)(2,1)S(1)} custom-call(s32[4]{0:T(128)S(1)} %pad_add_fusion.numbers_ref, bf16[512,3584]{1,0:T(8,128)(2,1)S(1)} %get-tuple-element.27.refs_0_, f32[512,128]{1,0:T(8,128)S(1)} %get-tuple-element.50.refs_1_.refs_5_, f32[512,128]{1,0:T(8,128)S(1)} %get-tuple-element.49.refs_2_.refs_6_, bf16[3584,1024]{1,0:T(8,128)(2,1)S(1)} %bitcast.9), custom_call_target="tpu_custom_call" | custom-call | flops 1879048192 | bytes 12058624 | tf_op jit(solution)/shard_map/pallas_call | solution.py:94
  23.5 3.8 %collective-permute-start.3 = (bf16[512,512]{1,0:T(8,128)(2,1)S(1)}, bf16[512,512]{1,0:T(8,128)(2,1)S(1)}, u32[]{:S(2)}, u32[]{:S(2)}) collective-permute-start(bf16[512,512]{1,0:T(8,128)(2,1)S(1)} %shard_map.76), channel_id=1, source_target_pairs={{0,2},{1,4},{2,0},{3,6},{4,3},{5,5},{6,1},{7,7},{8,10},{9,12},{10,... | collective-permute-start | bytes 1572872 | tf_op jit(solution)/shard_map/ppermute | solution.py:459
  27.3 2.6 %shard_map.75 = bf16[512,512]{1,0:T(8,128)(2,1)S(1)} custom-call(s32[4]{0:T(128)S(1)} %pad_add_fusion.numbers_ref, bf16[512,3584]{1,0:T(8,128)(2,1)S(1)} %get-tuple-element.27.refs_0_, f32[512,128]{1,0:T(8,128)S(1)} %get-tuple-element.50.refs_1_.refs_5_, f32[512,128]{1,0:T(8,128)S(1)} %get-tuple-element.49.refs_2_.refs_6_, bf16[3584,1024]{1,0:T(8,128)(2,1)S(1)} %bitcast.9), custom_call_target="tpu_custom_call" | custom-call | flops 1879048192 | bytes 12058624 | tf_op jit(solution)/shard_map/pallas_call | solution.py:94
  30.0 2.8 %collective-permute-start.2 = (bf16[512,512]{1,0:T(8,128)(2,1)S(1)}, bf16[512,512]{1,0:T(8,128)(2,1)S(1)}, u32[]{:S(2)}, u32[]{:S(2)}) collective-permute-start(bf16[512,512]{1,0:T(8,128)(2,1)S(1)} %shard_map.75), channel_id=1, source_target_pairs={{0,0},{1,6},{2,2},{3,4},{4,1},{5,7},{6,3},{7,5},{8,8},{9,14},{10,1... | collective-permute-start | bytes 1572872 | tf_op jit(solution)/shard_map/ppermute | solution.py:459
  32.8 0.0 collective-permute-done.8
  32.8 4.0 %collective-permute-start.9 = (bf16[512,512]{1,0:T(8,128)(2,1)S(1)}, bf16[512,512]{1,0:T(8,128)(2,1)S(1)}, u32[]{:S(2)}, u32[]{:S(2)}) collective-permute-start(bf16[512,512]{1,0:T(8,128)(2,1)S(1)} %collective-permute-done.8), channel_id=1, source_target_pairs={{0,0},{1,6},{2,2},{3,4},{4,1},{5,7},{6,3},{7,5},{8,8},{9,14},{10,1... | collective-permute-start | bytes 1572872 | tf_op jit(solution)/shard_map/ppermute | solution.py:459
  36.8 5.0 %collective-permute-done.4 = bf16[512,512]{1,0:T(8,128)(2,1)S(1)} collective-permute-done((bf16[512,512]{1,0:T(8,128)(2,1)S(1)}, bf16[512,512]{1,0:T(8,128)(2,1)S(1)}, u32[]{:S(2)}, u32[]{:S(2)}) %collective-permute-start.4) | collective-permute-done | bytes 524320 | tf_op jit(solution)/shard_map/ppermute | solution.py:446
  41.9 4.4 %collective-permute-start.5 = (bf16[512,512]{1,0:T(8,128)(2,1)S(1)}, bf16[512,512]{1,0:T(8,128)(2,1)S(1)}, u32[]{:S(2)}, u32[]{:S(2)}) collective-permute-start(bf16[512,512]{1,0:T(8,128)(2,1)S(1)} %collective-permute-done.4), channel_id=1, source_target_pairs={{0,2},{1,4},{2,0},{3,6},{4,3},{5,5},{6,1},{7,7},{8,10},{9,12},{10,... | collective-permute-start | bytes 1572872 | tf_op jit(solution)/shard_map/ppermute | solution.py:459
  46.2 0.0 collective-permute-done.3.refs_1_
  46.2 2.8 %collective-permute-start.14 = (bf16[512,512]{1,0:T(8,128)(2,1)S(1)}, bf16[512,512]{1,0:T(8,128)(2,1)S(1)}, u32[]{:S(2)}, u32[]{:S(2)}) collective-permute-start(bf16[512,512]{1,0:T(8,128)(2,1)S(1)} %get-tuple-element.29), channel_id=1, source_target_pairs={{0,0},{1,6},{2,2},{3,4},{4,1},{5,7},{6,3},{7,5},{8,8},{9,14},{10,1... | collective-permute-start | bytes 1572872 | tf_op jit(solution)/shard_map/ppermute | solution.py:459
  49.1 2.7 %collective-permute-start.12 = (bf16[512,512]{1,0:T(8,128)(2,1)S(1)}, bf16[512,512]{1,0:T(8,128)(2,1)S(1)}, u32[]{:S(2)}, u32[]{:S(2)}) collective-permute-start(bf16[512,512]{1,0:T(8,128)(2,1)S(1)} %get-tuple-element.28), channel_id=1, source_target_pairs={{0,2},{1,4},{2,0},{3,6},{4,3},{5,5},{6,1},{7,7},{8,10},{9,12},{10,... | collective-permute-start | bytes 1572872 | tf_op jit(solution)/shard_map/ppermute | solution.py:459
  51.8 0.1 collective-permute-start.17
  51.9 7.3 %collective-permute-done.5.refs_2_ = bf16[512,512]{1,0:T(8,128)(2,1)S(1)} collective-permute-done((bf16[512,512]{1,0:T(8,128)(2,1)S(1)}, bf16[512,512]{1,0:T(8,128)(2,1)S(1)}, u32[]{:S(2)}, u32[]{:S(2)}) %collective-permute-start.5) | collective-permute-done | bytes 524320 | tf_op jit(solution)/shard_map/ppermute | solution.py:459
  59.2 7.7 %collective-permute-done.14.refs_2_ = bf16[512,512]{1,0:T(8,128)(2,1)S(1)} collective-permute-done((bf16[512,512]{1,0:T(8,128)(2,1)S(1)}, bf16[512,512]{1,0:T(8,128)(2,1)S(1)}, u32[]{:S(2)}, u32[]{:S(2)}) %collective-permute-start.14) | collective-permute-done | bytes 524320 | tf_op jit(solution)/shard_map/ppermute | solution.py:459
  66.9 3.2 %collective-permute-start.10 = (bf16[512,512]{1,0:T(8,128)(2,1)S(1)}, bf16[512,512]{1,0:T(8,128)(2,1)S(1)}, u32[]{:S(2)}, u32[]{:S(2)}) collective-permute-start(bf16[512,512]{1,0:T(8,128)(2,1)S(1)} %collective-permute-done.9.refs_2_), channel_id=1, source_target_pairs={{0,8},{2,10},{4,12},{6,14},{8,16},{10,18},{12,20},{14,22},{16,24},... | collective-permute-start | bytes 1572872 | tf_op jit(solution)/shard_map/ppermute | solution.py:446
  70.1 0.0 collective-permute-done.12.refs_2_
  70.1 1.9 %collective-permute-start.6 = (bf16[512,512]{1,0:T(8,128)(2,1)S(1)}, bf16[512,512]{1,0:T(8,128)(2,1)S(1)}, u32[]{:S(2)}, u32[]{:S(2)}) collective-permute-start(bf16[512,512]{1,0:T(8,128)(2,1)S(1)} %collective-permute-done.5.refs_2_), channel_id=1, source_target_pairs={{0,8},{2,10},{4,12},{6,14},{8,16},{10,18},{12,20},{14,22},{16,24},... | collective-permute-start | bytes 1572872 | tf_op jit(solution)/shard_map/ppermute | solution.py:446
  72.0 0.0 collective-permute-done.17.refs_3_
  72.0 0.1 collective-permute-start.15
  72.1 0.0 collective-permute-done.16.refs_3_
  72.1 0.5 collective-permute-start.13
  72.6 8.9 %collective-permute-done.10.refs_2_ = bf16[512,512]{1,0:T(8,128)(2,1)S(1)} collective-permute-done((bf16[512,512]{1,0:T(8,128)(2,1)S(1)}, bf16[512,512]{1,0:T(8,128)(2,1)S(1)}, u32[]{:S(2)}, u32[]{:S(2)}) %collective-permute-start.10) | collective-permute-done | bytes 524320 | tf_op jit(solution)/shard_map/ppermute | solution.py:446
  81.5 0.0 collective-permute-start.11
  81.5 3.4 %shard_map.78 = (f32[2,512,512]{2,1,0:T(8,128)S(1)}, f32[2,512,256]{2,1,0:T(8,128)S(1)}) custom-call(s32[4]{0:T(128)S(1)} %pad_add_fusion.numbers_ref, bf16[512,512]{1,0:T(8,128)(2,1)S(1)} %collective-permute-done.2.refs_0_, bf16[512,512]{1,0:T(8,128)(2,1)S(1)} %collective-permute-done.3.refs_1_, bf16[512,512]{1,0:T(8,128)(2,1)S(1)} %collective-permute-done.9.refs_2_, ...), custom_call_target="tpu_custom_call" | custom-call | flops 1431655808 | bytes 5242880 | tf_op jit(solution)/shard_map/pallas_call | solution.py:94
  84.9 2.2 %collective-permute-done.6.refs_2_ = bf16[512,512]{1,0:T(8,128)(2,1)S(1)} collective-permute-done((bf16[512,512]{1,0:T(8,128)(2,1)S(1)}, bf16[512,512]{1,0:T(8,128)(2,1)S(1)}, u32[]{:S(2)}, u32[]{:S(2)}) %collective-permute-start.6) | collective-permute-done | bytes 524320 | tf_op jit(solution)/shard_map/ppermute | solution.py:446
  87.1 3.4 %shard_map.79 = (f32[2,512,512]{2,1,0:T(8,128)S(1)}, f32[2,512,256]{2,1,0:T(8,128)S(1)}) custom-call(s32[4]{0:T(128)S(1)} %pad_add_fusion.numbers_ref, bf16[512,512]{1,0:T(8,128)(2,1)S(1)} %collective-permute-done.2.refs_0_, bf16[512,512]{1,0:T(8,128)(2,1)S(1)} %collective-permute-done.3.refs_1_, ...), custom_call_target="tpu_custom_call", output_to_operand_aliasing={{0}: (5, {}), {1}: (6, {})} | custom-call | flops 1431655808 | bytes 8388608 | tf_op jit(solution)/shard_map/pallas_call | solution.py:94
  90.5 0.0 collective-permute-done.15.refs_3_
  90.5 4.4 %shard_map.80 = (f32[2,512,512]{2,1,0:T(8,128)S(1)}, f32[2,512,256]{2,1,0:T(8,128)S(1)}) custom-call(s32[4]{0:T(128)S(1)} %pad_add_fusion.numbers_ref, bf16[512,512]{1,0:T(8,128)(2,1)S(1)} %collective-permute-done.2.refs_0_, bf16[512,512]{1,0:T(8,128)(2,1)S(1)} %collective-permute-done.3.refs_1_, ...), custom_call_target="tpu_custom_call", output_to_operand_aliasing={{0}: (5, {}), {1}: (6, {})} | custom-call | flops 1431655808 | bytes 8388608 | tf_op jit(solution)/shard_map/pallas_call | solution.py:94
  94.9 0.0 collective-permute-done.13.refs_3_
  94.9 3.3 %shard_map.81 = (f32[2,512,512]{2,1,0:T(8,128)S(1)}, f32[2,512,256]{2,1,0:T(8,128)S(1)}) custom-call(s32[4]{0:T(128)S(1)} %pad_add_fusion.numbers_ref, bf16[512,512]{1,0:T(8,128)(2,1)S(1)} %collective-permute-done.2.refs_0_, bf16[512,512]{1,0:T(8,128)(2,1)S(1)} %collective-permute-done.3.refs_1_, ...), custom_call_target="tpu_custom_call", output_to_operand_aliasing={{0}: (5, {}), {1}: (6, {})} | custom-call | flops 1431655808 | bytes 8388608 | tf_op jit(solution)/shard_map/pallas_call | solution.py:94
  98.2 2.4 %shard_map.82 = (f32[2,512,512]{2,1,0:T(8,128)S(1)}, f32[2,512,256]{2,1,0:T(8,128)S(1)}, bf16[1024,1792]{1,0:T(8,128)(2,1)S(1)}, bf16[1024,1792]{1,0:T(8,128)(2,1)S(1)}) custom-call(s32[4]{0:T(128)S(1)} %pad_add_fusion.numbers_ref, bf16[512,512]{1,0:T(8,128)(2,1)S(1)} %collective-permute-done.2.refs_0_, ...), custom_call_target="tpu_custom_call", output_to_operand_aliasing={{0}: (5, {}), {1}: (6, {})} | custom-call | flops 1431655808 | bytes 8388608 | tf_op jit(solution)/shard_map/pallas_call | solution.py:94
  100.6 3.0 %shard_map.83 = (f32[2,512,512]{2,1,0:T(8,128)S(1)}, f32[2,512,256]{2,1,0:T(8,128)S(1)}) custom-call(s32[4]{0:T(128)S(1)} %pad_add_fusion.numbers_ref, bf16[512,512]{1,0:T(8,128)(2,1)S(1)} %collective-permute-done.2.refs_0_, bf16[512,512]{1,0:T(8,128)(2,1)S(1)} %collective-permute-done.3.refs_1_, ...), custom_call_target="tpu_custom_call", output_to_operand_aliasing={{0}: (4, {}), {1}: (5, {})} | custom-call | flops 715827904 | bytes 7864320 | tf_op jit(solution)/shard_map/pallas_call | solution.py:94
  103.6 1.1 shard_map.84
  104.7 1.9 %collective-permute-start.21 = (bf16[512,512]{1,0:T(8,128)(2,1)S(1)}, bf16[512,512]{1,0:T(8,128)(2,1)S(1)}, u32[]{:S(2)}, u32[]{:S(2)}) collective-permute-start(bf16[512,512]{1,0:T(8,128)(2,1)S(1)} %get-tuple-element.45), channel_id=1, source_target_pairs={{0,0},{6,1},{2,2},{4,3},{1,4},{7,5},{3,6},{5,7},{8,8},{14,9},{10,1... | collective-permute-start | bytes 1572872 | tf_op jit(solution)/shard_map/ppermute | solution.py:462
  106.7 4.5 %collective-permute-start.19 = (bf16[512,512]{1,0:T(8,128)(2,1)S(1)}, bf16[512,512]{1,0:T(8,128)(2,1)S(1)}, u32[]{:S(2)}, u32[]{:S(2)}) collective-permute-start(bf16[512,512]{1,0:T(8,128)(2,1)S(1)} %get-tuple-element.43), channel_id=1, source_target_pairs={{2,0},{4,1},{0,2},{6,3},{3,4},{5,5},{1,6},{7,7},{10,8},{12,9},{8,1... | collective-permute-start | bytes 1572872 | tf_op jit(solution)/shard_map/ppermute | solution.py:462
  111.2 8.6 %collective-permute-done.21.refs_0_ = bf16[512,512]{1,0:T(8,128)(2,1)S(1)} collective-permute-done((bf16[512,512]{1,0:T(8,128)(2,1)S(1)}, bf16[512,512]{1,0:T(8,128)(2,1)S(1)}, u32[]{:S(2)}, u32[]{:S(2)}) %collective-permute-start.21) | collective-permute-done | bytes 524320 | tf_op jit(solution)/shard_map/ppermute | solution.py:462
  119.8 2.9 %collective-permute-done.19.refs_0_ = bf16[512,512]{1,0:T(8,128)(2,1)S(1)} collective-permute-done((bf16[512,512]{1,0:T(8,128)(2,1)S(1)}, bf16[512,512]{1,0:T(8,128)(2,1)S(1)}, u32[]{:S(2)}, u32[]{:S(2)}) %collective-permute-start.19) | collective-permute-done | bytes 524320 | tf_op jit(solution)/shard_map/ppermute | solution.py:462
  122.7 0.0 collective-permute-start.20
  122.7 2.6 %shard_map.85.refs_3_ = f32[512,1792]{1,0:T(8,128)S(1)} custom-call(s32[4]{0:T(128)S(1)} %pad_add_fusion.numbers_ref, bf16[512,512]{1,0:T(8,128)(2,1)S(1)} %collective-permute-done.21.refs_0_, bf16[512,512]{1,0:T(8,128)(2,1)S(1)} %collective-permute-done.22.refs_1_, bf16[1024,1792]{1,0:T(8,128)(2,1)S(1)} %get-tuple-element.46.refs_2_), custom_call_target="tpu_custom_call" | custom-call | flops 1879048192 | bytes 8388608 | tf_op jit(solution)/shard_map/pallas_call | solution.py:94
  125.3 0.0 collective-permute-done.20.refs_1_
  125.3 0.0 copy-start.6
  125.4 3.2 %shard_map.86 = (f32[512,1792]{1,0:T(8,128)S(1)}, f32[512,128]{1,0:T(8,128)S(1)}) custom-call(s32[4]{0:T(128)S(1)} %pad_add_fusion.numbers_ref, bf16[512,512]{1,0:T(8,128)(2,1)S(1)} %collective-permute-done.19.refs_0_, bf16[512,512]{1,0:T(8,128)(2,1)S(1)} %collective-permute-done.20.refs_1_, ...), custom_call_target="tpu_custom_call", output_to_operand_aliasing={{0}: (4, {})} | custom-call | flops 1879048192 | bytes 12320768 | tf_op jit(solution)/shard_map/pallas_call | solution.py:94
  128.5 0.6 collective-permute-start.23
  129.1 1.2 collective-permute-done.23.refs_1_
  130.3 2.5 %shard_map.87 = bf16[512,1792]{1,0:T(8,128)(2,1)} custom-call(bf16[512,1792]{1,0:T(8,128)(2,1)S(1)} %copy-done.3, f32[512,1792]{1,0:T(8,128)S(1)} %get-tuple-element.47.share, f32[14,128]{1,0:T(8,128)S(1)} %bitcast.13, f32[512,128]{1,0:T(8,128)S(1)} %get-tuple-element.48.refs_0_, f32[512,128]{1,0:T(8,128)S(1)} %collective-permute-done.23.refs_1_), custom_call_target="tpu_custom_call" | custom-call | flops 7340032 | bytes 7340032 | tf_op jit(solution)/shard_map/pallas_call | solution.py:298
  (27 shorter events, 0.1 us)
Async XLA Ops:
  0.0 7.6 %collective-permute-start = (bf16[512,1792]{1,0:T(8,128)(2,1)}, bf16[512,1792]{1,0:T(8,128)(2,1)S(1)}, u32[]{:S(2)}, u32[]{:S(2)}) collective-permute-start(bf16[512,1792]{1,0:T(8,128)(2,1)} %tokens.1), channel_id=1, source_target_pairs={{0,1},{1,0},{2,3},{3,2},{4,5},{5,4},{6,7},{7,6},{8,9},{9,8},{10,11... | collective-permute-start | bytes 5505032 | tf_op jit(solution)/shard_map/ppermute | solution.py:443
  1.8 10.9 %slice-start = ((s8[7340032]{0:T(1024)(128)(4,1)}), s8[4194304]{0:T(1024)(128)(4,1)S(1)}, s32[]{:S(2)}) async-start(s8[7340032]{0:T(1024)(128)(4,1)} %bitcast.6), calls=%async_computation | async-start | bytes 8388608
  1.8 1.7 %copy-start.2 = (bf16[512,1792]{1,0:T(8,128)(2,1)S(1)}, bf16[512,1792]{1,0:T(8,128)(2,1)}, u32[]{:S(2)}) copy-start(bf16[512,1792]{1,0:T(8,128)(2,1)} %tokens.1) | copy-start | bytes 5505028
  3.4 0.9 copy-start.4
  4.3 0.7 copy-start.5
  5.0 2.6 %copy-start = (bf16[3584,512]{1,0:T(8,128)(2,1)S(1)}, bf16[3584,512]{1,0:T(8,128)(2,1)}, u32[]{:S(2)}) copy-start(bf16[3584,512]{1,0:T(8,128)(2,1)} %refs_3_.5) | copy-start | bytes 11010052
  5.0 3.2 %copy-start.1 = (bf16[3584,512]{1,0:T(8,128)(2,1)S(1)}, bf16[3584,512]{1,0:T(8,128)(2,1)}, u32[]{:S(2)}) copy-start(bf16[3584,512]{1,0:T(8,128)(2,1)} %refs_4_.1) | copy-start | bytes 11010052
  5.0 3.7 %copy-start.3 = (bf16[512,1792]{1,0:T(8,128)(2,1)S(1)}, bf16[512,1792]{1,0:T(8,128)(2,1)}, u32[]{:S(2)}) copy-start(bf16[512,1792]{1,0:T(8,128)(2,1)} %tokens.1) | copy-start | bytes 5505028
  5.0 7.7 %slice-start.1 = ((s8[7340032]{0:T(1024)(128)(4,1)}), s8[3145728]{0:T(1024)(128)(4,1)S(1)}, s32[]{:S(2)}) async-start(s8[7340032]{0:T(1024)(128)(4,1)} %bitcast.6), calls=%async_computation.1 | async-start | bytes 6291456
  6.0 1.6 %collective-permute-start.1 = (f32[512,128]{1,0:T(8,128)S(1)}, f32[512,128]{1,0:T(8,128)S(1)}, u32[]{:S(2)}, u32[]{:S(2)}) collective-permute-start(f32[512,128]{1,0:T(8,128)S(1)} %shard_map.73.refs_2_), channel_id=1, source_target_pairs={{0,1},{1,0},{2,3},{3,2},{4,5},{5,4},{6,7},{7,6},{8,9},{9,8},{10,11... | collective-permute-start | bytes 786440 | tf_op jit(solution)/shard_map/ppermute | solution.py:443
  12.7 8.2 %slice-start.2 = ((s8[7340032]{0:T(1024)(128)(4,1)}), s8[4194304]{0:T(1024)(128)(4,1)S(1)}, s32[]{:S(2)}) async-start(s8[7340032]{0:T(1024)(128)(4,1)} %bitcast.8), calls=%async_computation.2 | async-start | bytes 8388608
  12.7 8.1 %slice-start.3 = ((s8[7340032]{0:T(1024)(128)(4,1)}), s8[3145728]{0:T(1024)(128)(4,1)S(1)}, s32[]{:S(2)}) async-start(s8[7340032]{0:T(1024)(128)(4,1)} %bitcast.8), calls=%async_computation.3 | async-start | bytes 6291456
  15.6 82.6 %collective-permute-start.18 = (bf16[1024,1792]{1,0:T(8,128)(2,1)S(1)}, bf16[1024,1792]{1,0:T(8,128)(2,1)S(1)}, u32[]{:S(2)}, u32[]{:S(2)}) collective-permute-start(bf16[1024,1792]{1,0:T(8,128)(2,1)S(1)} %get-tuple-element.38), channel_id=1, source_target_pairs={{0,1},{1,0},{2,3},{3,2},{4,5},{5,4},{6,7},{7,6},{8,9},{9,8},{10,11... | collective-permute-start | bytes 11010056 | tf_op jit(solution)/shard_map/ppermute | solution.py:443
  15.7 17.1 %collective-permute-start.8 = (bf16[512,512]{1,0:T(8,128)(2,1)S(1)}, bf16[512,512]{1,0:T(8,128)(2,1)S(1)}, u32[]{:S(2)}, u32[]{:S(2)}) collective-permute-start(bf16[512,512]{1,0:T(8,128)(2,1)S(1)} %get-tuple-element.29), channel_id=1, source_target_pairs={{0,8},{2,10},{4,12},{6,14},{8,16},{10,18},{12,20},{14,22},{16,24},... | collective-permute-start | bytes 1572872 | tf_op jit(solution)/shard_map/ppermute | solution.py:446
  18.9 22.9 %collective-permute-start.4 = (bf16[512,512]{1,0:T(8,128)(2,1)S(1)}, bf16[512,512]{1,0:T(8,128)(2,1)S(1)}, u32[]{:S(2)}, u32[]{:S(2)}) collective-permute-start(bf16[512,512]{1,0:T(8,128)(2,1)S(1)} %get-tuple-element.28), channel_id=1, source_target_pairs={{0,8},{2,10},{4,12},{6,14},{8,16},{10,18},{12,20},{14,22},{16,24},... | collective-permute-start | bytes 1572872 | tf_op jit(solution)/shard_map/ppermute | solution.py:446
  23.5 22.7 %collective-permute-start.3 = (bf16[512,512]{1,0:T(8,128)(2,1)S(1)}, bf16[512,512]{1,0:T(8,128)(2,1)S(1)}, u32[]{:S(2)}, u32[]{:S(2)}) collective-permute-start(bf16[512,512]{1,0:T(8,128)(2,1)S(1)} %shard_map.76), channel_id=1, source_target_pairs={{0,2},{1,4},{2,0},{3,6},{4,3},{5,5},{6,1},{7,7},{8,10},{9,12},{10,... | collective-permute-start | bytes 1572872 | tf_op jit(solution)/shard_map/ppermute | solution.py:459
  30.0 19.1 %collective-permute-start.2 = (bf16[512,512]{1,0:T(8,128)(2,1)S(1)}, bf16[512,512]{1,0:T(8,128)(2,1)S(1)}, u32[]{:S(2)}, u32[]{:S(2)}) collective-permute-start(bf16[512,512]{1,0:T(8,128)(2,1)S(1)} %shard_map.75), channel_id=1, source_target_pairs={{0,0},{1,6},{2,2},{3,4},{4,1},{5,7},{6,3},{7,5},{8,8},{9,14},{10,1... | collective-permute-start | bytes 1572872 | tf_op jit(solution)/shard_map/ppermute | solution.py:459
  32.8 19.0 %collective-permute-start.9 = (bf16[512,512]{1,0:T(8,128)(2,1)S(1)}, bf16[512,512]{1,0:T(8,128)(2,1)S(1)}, u32[]{:S(2)}, u32[]{:S(2)}) collective-permute-start(bf16[512,512]{1,0:T(8,128)(2,1)S(1)} %collective-permute-done.8), channel_id=1, source_target_pairs={{0,0},{1,6},{2,2},{3,4},{4,1},{5,7},{6,3},{7,5},{8,8},{9,14},{10,1... | collective-permute-start | bytes 1572872 | tf_op jit(solution)/shard_map/ppermute | solution.py:459
  41.9 17.3 %collective-permute-start.5 = (bf16[512,512]{1,0:T(8,128)(2,1)S(1)}, bf16[512,512]{1,0:T(8,128)(2,1)S(1)}, u32[]{:S(2)}, u32[]{:S(2)}) collective-permute-start(bf16[512,512]{1,0:T(8,128)(2,1)S(1)} %collective-permute-done.4), channel_id=1, source_target_pairs={{0,2},{1,4},{2,0},{3,6},{4,3},{5,5},{6,1},{7,7},{8,10},{9,12},{10,... | collective-permute-start | bytes 1572872 | tf_op jit(solution)/shard_map/ppermute | solution.py:459
  46.2 20.7 %collective-permute-start.14 = (bf16[512,512]{1,0:T(8,128)(2,1)S(1)}, bf16[512,512]{1,0:T(8,128)(2,1)S(1)}, u32[]{:S(2)}, u32[]{:S(2)}) collective-permute-start(bf16[512,512]{1,0:T(8,128)(2,1)S(1)} %get-tuple-element.29), channel_id=1, source_target_pairs={{0,0},{1,6},{2,2},{3,4},{4,1},{5,7},{6,3},{7,5},{8,8},{9,14},{10,1... | collective-permute-start | bytes 1572872 | tf_op jit(solution)/shard_map/ppermute | solution.py:459
  49.1 21.0 %collective-permute-start.12 = (bf16[512,512]{1,0:T(8,128)(2,1)S(1)}, bf16[512,512]{1,0:T(8,128)(2,1)S(1)}, u32[]{:S(2)}, u32[]{:S(2)}) collective-permute-start(bf16[512,512]{1,0:T(8,128)(2,1)S(1)} %get-tuple-element.28), channel_id=1, source_target_pairs={{0,2},{1,4},{2,0},{3,6},{4,3},{5,5},{6,1},{7,7},{8,10},{9,12},{10,... | collective-permute-start | bytes 1572872 | tf_op jit(solution)/shard_map/ppermute | solution.py:459
  51.8 20.2 %collective-permute-start.17 = (bf16[512,512]{1,0:T(8,128)(2,1)S(1)}, bf16[512,512]{1,0:T(8,128)(2,1)S(1)}, u32[]{:S(2)}, u32[]{:S(2)}) collective-permute-start(bf16[512,512]{1,0:T(8,128)(2,1)S(1)} %collective-permute-done.9.refs_2_), channel_id=1, source_target_pairs={{0,1},{1,0},{2,3},{3,2},{4,5},{5,4},{6,7},{7,6},{8,9},{9,8},{10,11... | collective-permute-start | bytes 1572872 | tf_op jit(solution)/shard_map/ppermute | solution.py:443
  59.2 13.0 %collective-permute-start.16 = (bf16[512,512]{1,0:T(8,128)(2,1)S(1)}, bf16[512,512]{1,0:T(8,128)(2,1)S(1)}, u32[]{:S(2)}, u32[]{:S(2)}) collective-permute-start(bf16[512,512]{1,0:T(8,128)(2,1)S(1)} %collective-permute-done.5.refs_2_), channel_id=1, source_target_pairs={{0,1},{1,0},{2,3},{3,2},{4,5},{5,4},{6,7},{7,6},{8,9},{9,8},{10,11... | collective-permute-start | bytes 1572872 | tf_op jit(solution)/shard_map/ppermute | solution.py:443
  66.9 14.6 %collective-permute-start.10 = (bf16[512,512]{1,0:T(8,128)(2,1)S(1)}, bf16[512,512]{1,0:T(8,128)(2,1)S(1)}, u32[]{:S(2)}, u32[]{:S(2)}) collective-permute-start(bf16[512,512]{1,0:T(8,128)(2,1)S(1)} %collective-permute-done.9.refs_2_), channel_id=1, source_target_pairs={{0,8},{2,10},{4,12},{6,14},{8,16},{10,18},{12,20},{14,22},{16,24},... | collective-permute-start | bytes 1572872 | tf_op jit(solution)/shard_map/ppermute | solution.py:446
  70.1 17.0 %collective-permute-start.6 = (bf16[512,512]{1,0:T(8,128)(2,1)S(1)}, bf16[512,512]{1,0:T(8,128)(2,1)S(1)}, u32[]{:S(2)}, u32[]{:S(2)}) collective-permute-start(bf16[512,512]{1,0:T(8,128)(2,1)S(1)} %collective-permute-done.5.refs_2_), channel_id=1, source_target_pairs={{0,8},{2,10},{4,12},{6,14},{8,16},{10,18},{12,20},{14,22},{16,24},... | collective-permute-start | bytes 1572872 | tf_op jit(solution)/shard_map/ppermute | solution.py:446
  72.0 18.5 %collective-permute-start.15 = (bf16[512,512]{1,0:T(8,128)(2,1)S(1)}, bf16[512,512]{1,0:T(8,128)(2,1)S(1)}, u32[]{:S(2)}, u32[]{:S(2)}) collective-permute-start(bf16[512,512]{1,0:T(8,128)(2,1)S(1)} %collective-permute-done.14.refs_2_), channel_id=1, source_target_pairs={{0,1},{1,0},{2,3},{3,2},{4,5},{5,4},{6,7},{7,6},{8,9},{9,8},{10,11... | collective-permute-start | bytes 1572872 | tf_op jit(solution)/shard_map/ppermute | solution.py:443
  72.1 22.8 %collective-permute-start.13 = (bf16[512,512]{1,0:T(8,128)(2,1)S(1)}, bf16[512,512]{1,0:T(8,128)(2,1)S(1)}, u32[]{:S(2)}, u32[]{:S(2)}) collective-permute-start(bf16[512,512]{1,0:T(8,128)(2,1)S(1)} %collective-permute-done.12.refs_2_), channel_id=1, source_target_pairs={{0,1},{1,0},{2,3},{3,2},{4,5},{5,4},{6,7},{7,6},{8,9},{9,8},{10,11... | collective-permute-start | bytes 1572872 | tf_op jit(solution)/shard_map/ppermute | solution.py:443
  81.5 16.7 %collective-permute-start.11 = (bf16[512,512]{1,0:T(8,128)(2,1)S(1)}, bf16[512,512]{1,0:T(8,128)(2,1)S(1)}, u32[]{:S(2)}, u32[]{:S(2)}) collective-permute-start(bf16[512,512]{1,0:T(8,128)(2,1)S(1)} %collective-permute-done.10.refs_2_), channel_id=1, source_target_pairs={{0,1},{1,0},{2,3},{3,2},{4,5},{5,4},{6,7},{7,6},{8,9},{9,8},{10,11... | collective-permute-start | bytes 1572872 | tf_op jit(solution)/shard_map/ppermute | solution.py:443
  87.1 16.5 %collective-permute-start.7 = (bf16[512,512]{1,0:T(8,128)(2,1)S(1)}, bf16[512,512]{1,0:T(8,128)(2,1)S(1)}, u32[]{:S(2)}, u32[]{:S(2)}) collective-permute-start(bf16[512,512]{1,0:T(8,128)(2,1)S(1)} %collective-permute-done.6.refs_2_), channel_id=1, source_target_pairs={{0,1},{1,0},{2,3},{3,2},{4,5},{5,4},{6,7},{7,6},{8,9},{9,8},{10,11... | collective-permute-start | bytes 1572872 | tf_op jit(solution)/shard_map/ppermute | solution.py:443
  104.7 15.1 %collective-permute-start.21 = (bf16[512,512]{1,0:T(8,128)(2,1)S(1)}, bf16[512,512]{1,0:T(8,128)(2,1)S(1)}, u32[]{:S(2)}, u32[]{:S(2)}) collective-permute-start(bf16[512,512]{1,0:T(8,128)(2,1)S(1)} %get-tuple-element.45), channel_id=1, source_target_pairs={{0,0},{6,1},{2,2},{4,3},{1,4},{7,5},{3,6},{5,7},{8,8},{14,9},{10,1... | collective-permute-start | bytes 1572872 | tf_op jit(solution)/shard_map/ppermute | solution.py:462
  106.7 16.1 %collective-permute-start.19 = (bf16[512,512]{1,0:T(8,128)(2,1)S(1)}, bf16[512,512]{1,0:T(8,128)(2,1)S(1)}, u32[]{:S(2)}, u32[]{:S(2)}) collective-permute-start(bf16[512,512]{1,0:T(8,128)(2,1)S(1)} %get-tuple-element.43), channel_id=1, source_target_pairs={{2,0},{4,1},{0,2},{6,3},{3,4},{5,5},{1,6},{7,7},{10,8},{12,9},{8,1... | collective-permute-start | bytes 1572872 | tf_op jit(solution)/shard_map/ppermute | solution.py:462
  119.8 2.9 %collective-permute-start.22 = (bf16[512,512]{1,0:T(8,128)(2,1)S(1)}, bf16[512,512]{1,0:T(8,128)(2,1)S(1)}, u32[]{:S(2)}, u32[]{:S(2)}) collective-permute-start(bf16[512,512]{1,0:T(8,128)(2,1)S(1)} %collective-permute-done.21.refs_0_), channel_id=1, source_target_pairs={{0,1},{1,0},{2,3},{3,2},{4,5},{5,4},{6,7},{7,6},{8,9},{9,8},{10,11... | collective-permute-start | bytes 1572872 | tf_op jit(solution)/shard_map/ppermute | solution.py:443
  122.7 2.6 %collective-permute-start.20 = (bf16[512,512]{1,0:T(8,128)(2,1)S(1)}, bf16[512,512]{1,0:T(8,128)(2,1)S(1)}, u32[]{:S(2)}, u32[]{:S(2)}) collective-permute-start(bf16[512,512]{1,0:T(8,128)(2,1)S(1)} %collective-permute-done.19.refs_0_), channel_id=1, source_target_pairs={{0,1},{1,0},{2,3},{3,2},{4,5},{5,4},{6,7},{7,6},{8,9},{9,8},{10,11... | collective-permute-start | bytes 1572872 | tf_op jit(solution)/shard_map/ppermute | solution.py:443
  125.3 4.9 %copy-start.6 = (f32[1792]{0:T(1024)S(1)}, f32[1792]{0:T(1024)}, u32[]{:S(2)}) copy-start(f32[1792]{0:T(1024)} %param.13) | copy-start | bytes 21508
  128.5 1.7 %collective-permute-start.23 = (f32[512,128]{1,0:T(8,128)S(1)}, f32[512,128]{1,0:T(8,128)S(1)}, u32[]{:S(2)}, u32[]{:S(2)}) collective-permute-start(f32[512,128]{1,0:T(8,128)S(1)} %get-tuple-element.48.refs_0_), channel_id=1, source_target_pairs={{0,1},{1,0},{2,3},{3,2},{4,5},{5,4},{6,7},{7,6},{8,9},{9,8},{10,11... | collective-permute-start | bytes 786440 | tf_op jit(solution)/shard_map/ppermute | solution.py:443
where the time goes:
time: 133 us
  waiting for transfers between devices  45.3 us (34%)
  Pallas kernels  42.4 us (32%)
  starting transfers between devices  39.3 us (30%)
  local copies, waits for them, and re-layouts  4.27 us (3%)
    pallas_call x14, Pallas kernels, kernel_call(): pl.pallas_call(kernel, out_shape=list(out_shape) + fetch.shapes(), in_spe...  39.9 us
    ppermute x6, starting transfers between devices, spread(): return lax.ppermute(value, ('seq', 'head'), route(turn))  20.6 us
    ppermute x4, waiting for transfers between devices, next_plane(): lax.ppermute(value, 'seq', [(i, i + plane) for i in range(n_seq - plane)])  16.1 us
    ppermute x6, waiting for transfers between devices, spread(): return lax.ppermute(value, ('seq', 'head'), route(turn))  15 us
    ppermute x2, waiting for transfers between devices, gather_back(): lax.ppermute(value, ('seq', 'head'), [(b, a) for a, b in route(turn)])  11.5 us
    ppermute x4, starting transfers between devices, next_plane(): lax.ppermute(value, 'seq', [(i, i + plane) for i in range(n_seq - plane)])  10.2 us
    ppermute x2, starting transfers between devices, gather_back(): lax.ppermute(value, ('seq', 'head'), [(b, a) for a, b in route(turn)])  6.46 us
    unnamed x22, local copies, waits for them, and re-layouts  4.27 us
  transfers between devices with their start and end apart: 24, of which 9 were waited for; matrix products, arithmetic and copies ran while one was open for 1% of the time, Pallas kernels for 22%

commit v1 on v0

--- a/solution.py
+++ b/solution.py
@@ -229,7 +229,7 @@
     return kernel_call(body, fetch, numbers, [normed, *tables, *weights], out, [], 8, flops)
 
 
-def out_projection(numbers, lefts, weight, total, last):
+def out_projection(numbers, lefts, weight, some, total, last):
     n = len(lefts)
     rows, width = lefts[0].shape
     out_width = weight.shape[1]
@@ -243,7 +243,7 @@
             left[:, k * width : (k + 1) * width] = inputs[k][...]
         for column in range(0, out_width, columns):
             here = slice(column, column + columns)
-            value = dot(left[...], weight_ref[:, here])
+            value = dot(left[...], weight_ref[some[0] * width : (some[-1] + 1) * width, here])
             if total is not None:
                 value = value + inputs[n + 1][:, here]
             outputs[0][:, here] = value
@@ -316,23 +316,22 @@
     lanes = min(128, rows)
     window_blocks = WINDOW // rows
     first = totals is None
-    acc_shape = (n_q, rows, width)
-    den_shape = (n_q, rows, heads * lanes)
+    shapes = [(rows, width)] * n_q + [(rows, heads * lanes)] * n_q
     chunk = min(ROW_CHUNK, rows)
 
     def body(scalars, inputs, outputs, scratch):
         q_refs, kv_refs = inputs[:n_q], inputs[n_q : n_q + n_kv]
         kv_all, key_numbers = scratch[:2]
-        acc, den = scratch[2:] if last else outputs
+        state = scratch[2:] if last else outputs
+        acc, den = state[:n_q], state[n_q:]
         for k in range(n_kv):
             kv_all[k * rows : (k + 1) * rows, :] = kv_refs[k][...]
             key_numbers[k] = key_blocks[k](scalars)
-        if first:
-            acc[...] = jnp.zeros_like(acc)
-            den[...] = jnp.zeros_like(den)
-        elif last:
-            acc[...] = inputs[n_q + n_kv][...]
-            den[...] = inputs[n_q + n_kv + 1][...]
+        for k, ref in enumerate(state):
+            if first:
+                ref[...] = jnp.zeros_like(ref)
+            elif last:
+                ref[...] = inputs[n_q + n_kv + k][...]
 
         def add(r, keys_at, delta):
             for head in range(heads):
@@ -350,16 +349,21 @@
                         * (softcap_limit * LOG2E)
                     )
                     if delta is not None:
-                        offset = (
+                        ahead = (
                             lax.broadcasted_iota(jnp.int32, weights.shape, 0)
                             - lax.broadcasted_iota(jnp.int32, weights.shape, 1)
-                            + (delta * rows + start)
+                            + start
                         )
-                        allowed = (offset >= 0) & (offset < window_blocks * rows)
-                        weights = jnp.where(allowed, weights, 0.0)
+                        limit = jnp.where((delta > 0) & (delta < window_blocks), -rows, 0)
+                        far = delta == window_blocks
+                        weights = weights * jnp.where(
+                            ahead >= limit,
+                            jnp.where(far, 0.0, 1.0).astype(jnp.float32),
+                            jnp.where(far, 1.0, 0.0).astype(jnp.float32),
+                        )
                     lane_at = slice(head * lanes, (head + 1) * lanes)
-                    den[r, at, lane_at] = den[r, at, lane_at] + lane_sums(weights, lanes)
-                    acc[r, at, columns] = acc[r, at, columns] + dot(
+                    den[r][at, lane_at] = den[r][at, lane_at] + lane_sums(weights, lanes)
+                    acc[r][at, columns] = acc[r][at, columns] + dot(
                         weights.astype(jnp.bfloat16), kv_all[keys_at, HD:]
                     )
 
@@ -399,10 +403,10 @@
             for r in range(n_q):
                 for head in range(heads):
                     total = jnp.sum(
-                        den[r, :, head * lanes : (head + 1) * lanes], axis=-1, keepdims=True
+                        den[r][:, head * lanes : (head + 1) * lanes], axis=-1, keepdims=True
                     )
                     columns = slice(head * HD, (head + 1) * HD)
-                    outputs[r][:, columns] = (acc[r, :, columns] / total).astype(jnp.bfloat16)
+                    outputs[r][:, columns] = (acc[r][:, columns] / total).astype(jnp.bfloat16)
 
     scratch = [
         pltpu.VMEM((n_kv * rows, pieces[0].shape[1]), jnp.bfloat16),
@@ -410,16 +414,12 @@
     ]
     operands = [*queries, *pieces] + ([] if first else list(totals))
     aliases = {}
+    out = [jax.ShapeDtypeStruct(shape, jnp.float32) for shape in shapes]
     if last:
+        scratch += [pltpu.VMEM(shape, jnp.float32) for shape in shapes]
         out = [jax.ShapeDtypeStruct((rows, width), jnp.bfloat16)] * n_q
-        scratch += [pltpu.VMEM(acc_shape, jnp.float32), pltpu.VMEM(den_shape, jnp.float32)]
-    else:
-        out = [
-            jax.ShapeDtypeStruct(acc_shape, jnp.float32),
-            jax.ShapeDtypeStruct(den_shape, jnp.float32),
-        ]
-        if not first:
-            aliases = {n_q + n_kv: 0, n_q + n_kv + 1: 1}
+    elif not first:
+        aliases = {n_q + n_kv + k: k for k in range(2 * n_q)}
     flops = n_q * n_kv * heads * 4 * rows * rows * HD * 2 // 3
     return kernel_call(body, fetch, numbers, operands, out, scratch, 14, flops, aliases)
 
@@ -540,9 +540,13 @@
 
     query_blocks = [block_of(0, turn, 0) for turn in turns]
 
+    merged = {}
+
     def piece_of(lag, turn, by):
-        piece = levels[lag][turn]
-        return over_cores(piece, by) if by else piece
+        if (lag, turn, by) not in merged:
+            piece = levels[lag][turn]
+            merged[lag, turn, by] = over_cores(piece, by) if by else piece
+        return merged[lag, turn, by]
 
     out_fetch = []
     for turn in turns:
@@ -559,30 +563,52 @@
                 )
             )
         out_fetch.append(((piece_width * cores, part), blocks))
-    calls = []
+    calls = [[(0, 0, by) for by in range(cores)]]
     for lag in range(1, hops + 1):
         for turn in turns:
             calls.append([(lag, turn, by) for by in range(cores)])
-        if lag == 1:
-            calls += [[(0, turn, by) for by in range(cores)] for turn in turns]
+    calls[-1:-1] = [[(0, turn, by) for by in range(cores)] for turn in turns[1:]]
     calls[-1:] = [calls[-1][:1], calls[-1][1:]]
-    totals = None
-    for index, call in enumerate(calls):
+    n_q = len(q_pieces)
+    totals, attended, out_blocks = None, [], None
+
+    def run(call, some, state, last, fetch):
         blocks = [block_of(by, turn, lag) for lag, turn, by in call]
         pieces = [piece_of(*key) for key in call]
-        last = index == len(calls) - 1
         full = all(0 < lag < hops for lag, _, _ in call)
-        fetch = Fetch(row_blocks, out_fetch) if index == len(calls) - 3 else NOTHING
-        totals = attend(numbers, query_blocks, blocks, q_pieces, pieces, totals, last, full, fetch)
+        return attend(
+            numbers,
+            [query_blocks[r] for r in some],
+            blocks,
+            [q_pieces[r] for r in some],
+            pieces,
+            state,
+            last,
+            full,
+            fetch,
+        )
+
+    for index, call in enumerate(calls[:-1]):
+        fetch = Fetch(row_blocks, out_fetch) if index == len(calls) - 5 else NOTHING
+        totals = run(call, range(n_q), totals, False, fetch)
         if fetch is not NOTHING:
-            totals, out_blocks = totals[:2], totals[2:]
-    attended = totals
+            totals, out_blocks = totals[: 2 * n_q], totals[2 * n_q :]
+    for r in range(n_q):
+        state = [totals[r], totals[n_q + r]]
+        attended += run(calls[-1], [r], state, True, NOTHING)
     total = None
     for turn, o in enumerate(attended):
         own = gather_back(o, turn)
         lefts = [own] + [over_cores(own, by) for by in others]
-        out = out_projection(numbers, lefts, out_blocks[turn], total, turn == kv_heads - 1)
-        total = out[0]
+        parts = [range(cores)]
+        if turn == kv_heads - 1:
+            parts = [range(1), range(1, cores)]
+        for index, some in enumerate(parts):
+            last = turn == kv_heads - 1 and index == len(parts) - 1
+            out = out_projection(
+                numbers, [lefts[k] for k in some], out_blocks[turn], some, total, last
+            )
+            total = out[0]
     share, own_squares = out
     squares = [own_squares] + [over_cores(own_squares, by) for by in others]
     return finish(tokens, share, gain_out, squares)

time: 133 us -> 131 us (0.985); the launches traced: 133 us -> 129 us
  waiting for transfers between devices: 45.3 us -> 40.9 us
    ppermute x6, waiting for transfers between devices: 15 us -> 10.1 us  [spread(): return lax.ppermute(value, ('seq', 'head'), route(turn))]
    pallas_call x14 -> x16, Pallas kernels: 39.9 us -> 40.9 us  [kernel_call(): pl.pallas_call(kernel, out_shape=list(out_shape) + fetch.shapes(), in_spe...]
  transfers between devices with their start and end apart: 24 -> 24, of which waited for: 9 -> 9; matrix products, arithmetic and copies ran while one was open for 1% -> 1% of each run, Pallas kernels for 22% -> 24%
where the time goes in v1:
time: 131 us; the launch traced here: 129 us
  Pallas kernels  43.4 us (33%)
  waiting for transfers between devices  40.9 us (31%)
  starting transfers between devices  39.2 us (30%)
  local copies, waits for them, and re-layouts  4.4 us (3%)
    pallas_call x16, Pallas kernels, kernel_call(): pl.pallas_call(kernel, out_shape=list(out_shape) + fetch.shapes(), in_spe...  40.9 us
    ppermute x6, starting transfers between devices, spread(): return lax.ppermute(value, ('seq', 'head'), route(turn))  20.2 us
    ppermute x4, waiting for transfers between devices, next_plane(): lax.ppermute(value, 'seq', [(i, i + plane) for i in range(n_seq - plane)])  17.1 us
    ppermute x2, waiting for transfers between devices, gather_back(): lax.ppermute(value, ('seq', 'head'), [(b, a) for a, b in route(turn)])  11.1 us
    ppermute x6, waiting for transfers between devices, spread(): return lax.ppermute(value, ('seq', 'head'), route(turn))  10.1 us
    ppermute x4, starting transfers between devices, next_plane(): lax.ppermute(value, 'seq', [(i, i + plane) for i in range(n_seq - plane)])  8.96 us
    ppermute x2, starting transfers between devices, gather_back(): lax.ppermute(value, ('seq', 'head'), [(b, a) for a, b in route(turn)])  7.34 us
    unnamed x22, local copies, waits for them, and re-layouts  4.4 us
  transfers between devices with their start and end apart: 24, of which 9 were waited for; matrix products, arithmetic and copies ran while one was open for 1% of the time, Pallas kernels for 24%

profile of v1, /device:TPU:17, one launch (start us, length us, event | category | flops | bytes accessed | tf_op | source)
XLA Modules:
  0.0 129.3 jit_solution(13538198701816217154)
XLA Ops:
  0.0 0.7 collective-permute-start
  0.7 1.0 multiply_sine_fusion
  1.7 0.1 pad_add_fusion.numbers_ref
  1.8 1.6 %copy-done.2 = bf16[512,1792]{1,0:T(8,128)(2,1)S(1)} copy-done((bf16[512,1792]{1,0:T(8,128)(2,1)S(1)}, bf16[512,1792]{1,0:T(8,128)(2,1)}, u32[]{:S(2)}) %copy-start.2) | copy-done | bytes 1835032
  3.4 0.9 copy-done.4
  4.3 0.7 copy-done.5
  5.0 1.0 shard_map.73.refs_2_
  6.0 0.1 collective-permute-start.1
  6.1 1.5 %collective-permute-done.1.refs_3_ = f32[512,128]{1,0:T(8,128)S(1)} collective-permute-done((f32[512,128]{1,0:T(8,128)S(1)}, f32[512,128]{1,0:T(8,128)S(1)}, u32[]{:S(2)}, u32[]{:S(2)}) %collective-permute-start.1) | collective-permute-done | bytes 262176 | tf_op jit(solution)/shard_map/ppermute | solution.py:443
  7.6 0.0 collective-permute-done.refs_1_
  7.7 0.5 copy-done.1
  8.2 0.5 copy-done.3
  8.7 4.0 %shard_map.74 = (bf16[512,3584]{1,0:T(8,128)(2,1)S(1)}, bf16[512,512]{1,0:T(8,128)(2,1)S(1)}) custom-call(s32[4]{0:T(128)S(1)} %pad_add_fusion.numbers_ref, bf16[512,1792]{1,0:T(8,128)(2,1)S(1)} %copy-done.3, bf16[512,1792]{1,0:T(8,128)(2,1)S(1)} %collective-permute-done.refs_1_, f32[512,128]{1,0:T(8,128)S(1)} %shard_map.73.refs_2_, ...), custom_call_target="tpu_custom_call" | custom-call | flops 1879048192 | bytes 16267264 | tf_op jit(solution)/shard_map/pallas_call | solution.py:94
  12.7 0.0 slice-start.2
  12.8 2.9 %shard_map.76 = (bf16[512,512]{1,0:T(8,128)(2,1)S(1)}, bf16[1024,1792]{1,0:T(8,128)(2,1)S(1)}) custom-call(s32[4]{0:T(128)S(1)} %pad_add_fusion.numbers_ref, bf16[512,3584]{1,0:T(8,128)(2,1)S(1)} %get-tuple-element.37.refs_0_, f32[512,128]{1,0:T(8,128)S(1)} %get-tuple-element.70.refs_1_.refs_5_, f32[512,128]{1,0:T(8,128)S(1)} %get-tuple-element.69.refs_2_.refs_6_, ...), custom_call_target="tpu_custom_call" | custom-call | flops 1879048192 | bytes 12058624 | tf_op jit(solution)/shard_map/pallas_call | solution.py:94
  15.6 0.1 collective-permute-start.18
  15.7 0.1 slice-done.3
  15.9 2.6 %shard_map.77 = bf16[512,512]{1,0:T(8,128)(2,1)S(1)} custom-call(s32[4]{0:T(128)S(1)} %pad_add_fusion.numbers_ref, bf16[512,3584]{1,0:T(8,128)(2,1)S(1)} %get-tuple-element.37.refs_0_, f32[512,128]{1,0:T(8,128)S(1)} %get-tuple-element.70.refs_1_.refs_5_, f32[512,128]{1,0:T(8,128)S(1)} %get-tuple-element.69.refs_2_.refs_6_, bf16[3584,1024]{1,0:T(8,128)(2,1)S(1)} %bitcast.9), custom_call_target="tpu_custom_call" | custom-call | flops 1879048192 | bytes 12058624 | tf_op jit(solution)/shard_map/pallas_call | solution.py:94
  18.5 4.3 %collective-permute-start.7 = (bf16[512,512]{1,0:T(8,128)(2,1)S(1)}, bf16[512,512]{1,0:T(8,128)(2,1)S(1)}, u32[]{:S(2)}, u32[]{:S(2)}) collective-permute-start(bf16[512,512]{1,0:T(8,128)(2,1)S(1)} %shard_map.77), channel_id=1, source_target_pairs={{0,0},{1,6},{2,2},{3,4},{4,1},{5,7},{6,3},{7,5},{8,8},{9,14},{10,1... | collective-permute-start | bytes 1572872 | tf_op jit(solution)/shard_map/ppermute | solution.py:459
  22.8 3.2 %collective-permute-start.10 = (bf16[512,512]{1,0:T(8,128)(2,1)S(1)}, bf16[512,512]{1,0:T(8,128)(2,1)S(1)}, u32[]{:S(2)}, u32[]{:S(2)}) collective-permute-start(bf16[512,512]{1,0:T(8,128)(2,1)S(1)} %get-tuple-element.39), channel_id=1, source_target_pairs={{0,8},{2,10},{4,12},{6,14},{8,16},{10,18},{12,20},{14,22},{16,24},... | collective-permute-start | bytes 1572872 | tf_op jit(solution)/shard_map/ppermute | solution.py:446
  26.0 2.5 %collective-permute-start.16 = (bf16[512,512]{1,0:T(8,128)(2,1)S(1)}, bf16[512,512]{1,0:T(8,128)(2,1)S(1)}, u32[]{:S(2)}, u32[]{:S(2)}) collective-permute-start(bf16[512,512]{1,0:T(8,128)(2,1)S(1)} %get-tuple-element.39), channel_id=1, source_target_pairs={{0,0},{1,6},{2,2},{3,4},{4,1},{5,7},{6,3},{7,5},{8,8},{9,14},{10,1... | collective-permute-start | bytes 1572872 | tf_op jit(solution)/shard_map/ppermute | solution.py:459
  28.5 1.9 %collective-permute-start.3 = (bf16[512,512]{1,0:T(8,128)(2,1)S(1)}, bf16[512,512]{1,0:T(8,128)(2,1)S(1)}, u32[]{:S(2)}, u32[]{:S(2)}) collective-permute-start(bf16[512,512]{1,0:T(8,128)(2,1)S(1)} %get-tuple-element.38), channel_id=1, source_target_pairs={{0,8},{2,10},{4,12},{6,14},{8,16},{10,18},{12,20},{14,22},{16,24},... | collective-permute-start | bytes 1572872 | tf_op jit(solution)/shard_map/ppermute | solution.py:446
  30.4 2.6 %shard_map.75 = bf16[512,512]{1,0:T(8,128)(2,1)S(1)} custom-call(s32[4]{0:T(128)S(1)} %pad_add_fusion.numbers_ref, bf16[512,3584]{1,0:T(8,128)(2,1)S(1)} %get-tuple-element.37.refs_0_, f32[512,128]{1,0:T(8,128)S(1)} %get-tuple-element.70.refs_1_.refs_5_, f32[512,128]{1,0:T(8,128)S(1)} %get-tuple-element.69.refs_2_.refs_6_, bf16[3584,1024]{1,0:T(8,128)(2,1)S(1)} %bitcast.9), custom_call_target="tpu_custom_call" | custom-call | flops 1879048192 | bytes 12058624 | tf_op jit(solution)/shard_map/pallas_call | solution.py:94
  33.1 0.0 collective-permute-done.7.refs_0_
  33.1 3.1 %collective-permute-start.2 = (bf16[512,512]{1,0:T(8,128)(2,1)S(1)}, bf16[512,512]{1,0:T(8,128)(2,1)S(1)}, u32[]{:S(2)}, u32[]{:S(2)}) collective-permute-start(bf16[512,512]{1,0:T(8,128)(2,1)S(1)} %shard_map.75), channel_id=1, source_target_pairs={{0,2},{1,4},{2,0},{3,6},{4,3},{5,5},{6,1},{7,7},{8,10},{9,12},{10,... | collective-permute-start | bytes 1572872 | tf_op jit(solution)/shard_map/ppermute | solution.py:459
  36.2 2.5 %collective-permute-done.10 = bf16[512,512]{1,0:T(8,128)(2,1)S(1)} collective-permute-done((bf16[512,512]{1,0:T(8,128)(2,1)S(1)}, bf16[512,512]{1,0:T(8,128)(2,1)S(1)}, u32[]{:S(2)}, u32[]{:S(2)}) %collective-permute-start.10) | collective-permute-done | bytes 524320 | tf_op jit(solution)/shard_map/ppermute | solution.py:446
  38.7 3.0 %collective-permute-start.11 = (bf16[512,512]{1,0:T(8,128)(2,1)S(1)}, bf16[512,512]{1,0:T(8,128)(2,1)S(1)}, u32[]{:S(2)}, u32[]{:S(2)}) collective-permute-start(bf16[512,512]{1,0:T(8,128)(2,1)S(1)} %collective-permute-done.10), channel_id=1, source_target_pairs={{0,0},{1,6},{2,2},{3,4},{4,1},{5,7},{6,3},{7,5},{8,8},{9,14},{10,1... | collective-permute-start | bytes 1572872 | tf_op jit(solution)/shard_map/ppermute | solution.py:459
  41.7 0.0 collective-permute-done.16.refs_2_
  41.7 2.5 %collective-permute-start.8 = (bf16[512,512]{1,0:T(8,128)(2,1)S(1)}, bf16[512,512]{1,0:T(8,128)(2,1)S(1)}, u32[]{:S(2)}, u32[]{:S(2)}) collective-permute-start(bf16[512,512]{1,0:T(8,128)(2,1)S(1)} %get-tuple-element.38), channel_id=1, source_target_pairs={{0,2},{1,4},{2,0},{3,6},{4,3},{5,5},{6,1},{7,7},{8,10},{9,12},{10,... | collective-permute-start | bytes 1572872 | tf_op jit(solution)/shard_map/ppermute | solution.py:459
  44.2 2.9 %collective-permute-done.3 = bf16[512,512]{1,0:T(8,128)(2,1)S(1)} collective-permute-done((bf16[512,512]{1,0:T(8,128)(2,1)S(1)}, bf16[512,512]{1,0:T(8,128)(2,1)S(1)}, u32[]{:S(2)}, u32[]{:S(2)}) %collective-permute-start.3) | collective-permute-done | bytes 524320 | tf_op jit(solution)/shard_map/ppermute | solution.py:446
  47.1 4.8 %collective-permute-start.4 = (bf16[512,512]{1,0:T(8,128)(2,1)S(1)}, bf16[512,512]{1,0:T(8,128)(2,1)S(1)}, u32[]{:S(2)}, u32[]{:S(2)}) collective-permute-start(bf16[512,512]{1,0:T(8,128)(2,1)S(1)} %collective-permute-done.3), channel_id=1, source_target_pairs={{0,2},{1,4},{2,0},{3,6},{4,3},{5,5},{6,1},{7,7},{8,10},{9,12},{10,... | collective-permute-start | bytes 1572872 | tf_op jit(solution)/shard_map/ppermute | solution.py:459
  51.9 0.0 collective-permute-done.2.refs_1_.refs_0_
  51.9 0.1 collective-permute-start.17
  52.0 10.0 %collective-permute-done.11.refs_2_ = bf16[512,512]{1,0:T(8,128)(2,1)S(1)} collective-permute-done((bf16[512,512]{1,0:T(8,128)(2,1)S(1)}, bf16[512,512]{1,0:T(8,128)(2,1)S(1)}, u32[]{:S(2)}, u32[]{:S(2)}) %collective-permute-start.11) | collective-permute-done | bytes 524320 | tf_op jit(solution)/shard_map/ppermute | solution.py:459
  62.0 1.9 %collective-permute-start.12 = (bf16[512,512]{1,0:T(8,128)(2,1)S(1)}, bf16[512,512]{1,0:T(8,128)(2,1)S(1)}, u32[]{:S(2)}, u32[]{:S(2)}) collective-permute-start(bf16[512,512]{1,0:T(8,128)(2,1)S(1)} %collective-permute-done.11.refs_2_), channel_id=1, source_target_pairs={{0,8},{2,10},{4,12},{6,14},{8,16},{10,18},{12,20},{14,22},{16,24},... | collective-permute-start | bytes 1572872 | tf_op jit(solution)/shard_map/ppermute | solution.py:446
  63.9 0.0 collective-permute-done.8.refs_2_
  64.0 0.1 collective-permute-start.15
  64.0 0.0 collective-permute-done.4.refs_2_
  64.0 1.9 %collective-permute-start.5 = (bf16[512,512]{1,0:T(8,128)(2,1)S(1)}, bf16[512,512]{1,0:T(8,128)(2,1)S(1)}, u32[]{:S(2)}, u32[]{:S(2)}) collective-permute-start(bf16[512,512]{1,0:T(8,128)(2,1)S(1)} %collective-permute-done.4.refs_2_), channel_id=1, source_target_pairs={{0,8},{2,10},{4,12},{6,14},{8,16},{10,18},{12,20},{14,22},{16,24},... | collective-permute-start | bytes 1572872 | tf_op jit(solution)/shard_map/ppermute | solution.py:446
  66.0 0.0 collective-permute-done.17.refs_3_
  66.0 0.5 collective-permute-start.14
  66.5 8.4 %collective-permute-done.12.refs_2_ = bf16[512,512]{1,0:T(8,128)(2,1)S(1)} collective-permute-done((bf16[512,512]{1,0:T(8,128)(2,1)S(1)}, bf16[512,512]{1,0:T(8,128)(2,1)S(1)}, u32[]{:S(2)}, u32[]{:S(2)}) %collective-permute-start.12) | collective-permute-done | bytes 524320 | tf_op jit(solution)/shard_map/ppermute | solution.py:446
  74.9 0.0 collective-permute-done.15.refs_3_
  74.9 0.5 collective-permute-start.9
  75.4 4.4 %shard_map.78 = (f32[512,512]{1,0:T(8,128)S(1)}, f32[512,512]{1,0:T(8,128)S(1)}, f32[512,256]{1,0:T(8,128)S(1)}, f32[512,256]{1,0:T(8,128)S(1)}) custom-call(s32[4]{0:T(128)S(1)} %pad_add_fusion.numbers_ref, bf16[512,512]{1,0:T(8,128)(2,1)S(1)} %collective-permute-done.7.refs_0_, bf16[512,512]{1,0:T(8,128)(2,1)S(1)} %collective-permute-done.2.refs_1_.refs_0_, ...), custom_call_target="tpu_custom_call" | custom-call | flops 1431655808 | bytes 5242880 | tf_op jit(solution)/shard_map/pallas_call | solution.py:94
  79.8 3.4 %collective-permute-done.5.refs_2_ = bf16[512,512]{1,0:T(8,128)(2,1)S(1)} collective-permute-done((bf16[512,512]{1,0:T(8,128)(2,1)S(1)}, bf16[512,512]{1,0:T(8,128)(2,1)S(1)}, u32[]{:S(2)}, u32[]{:S(2)}) %collective-permute-start.5) | collective-permute-done | bytes 524320 | tf_op jit(solution)/shard_map/ppermute | solution.py:446
  83.2 3.4 %shard_map.79 = (f32[512,512]{1,0:T(8,128)S(1)}, f32[512,512]{1,0:T(8,128)S(1)}, f32[512,256]{1,0:T(8,128)S(1)}, f32[512,256]{1,0:T(8,128)S(1)}) custom-call(s32[4]{0:T(128)S(1)} %pad_add_fusion.numbers_ref, bf16[512,512]{1,0:T(8,128)(2,1)S(1)} %collective-permute-done.7.refs_0_, ...), custom_call_target="tpu_custom_call", output_to_operand_aliasing={{0}: (5, {}), {1}: (6, {}), {2}: (7, {}), {3}: (8, {})} | custom-call | flops 1431655808 | bytes 8388608 | tf_op jit(solution)/shard_map/pallas_call | solution.py:94
  86.6 3.8 %shard_map.80 = (f32[512,512]{1,0:T(8,128)S(1)}, f32[512,512]{1,0:T(8,128)S(1)}, f32[512,256]{1,0:T(8,128)S(1)}, f32[512,256]{1,0:T(8,128)S(1)}, bf16[1024,1792]...) custom-call(s32[4]{0:T(128)S(1)} %pad_add_fusion.numbers_ref, ...), custom_call_target="tpu_custom_call", output_to_operand_aliasing={{0}: (5, {}), {1}: (6, {}), {2}: (7, {}), {3}: (8, {})} | custom-call | flops 1431655808 | bytes 8388608 | tf_op jit(solution)/shard_map/pallas_call | solution.py:94
  90.5 1.7 %shard_map.81 = (f32[512,512]{1,0:T(8,128)S(1)}, f32[512,512]{1,0:T(8,128)S(1)}, f32[512,256]{1,0:T(8,128)S(1)}, f32[512,256]{1,0:T(8,128)S(1)}) custom-call(s32[4]{0:T(128)S(1)} %pad_add_fusion.numbers_ref, bf16[512,512]{1,0:T(8,128)(2,1)S(1)} %collective-permute-done.7.refs_0_, ...), custom_call_target="tpu_custom_call", output_to_operand_aliasing={{0}: (5, {}), {1}: (6, {}), {2}: (7, {}), {3}: (8, {})} | custom-call | flops 1431655808 | bytes 8388608 | tf_op jit(solution)/shard_map/pallas_call | solution.py:94
  92.2 3.2 %shard_map.82 = (f32[512,512]{1,0:T(8,128)S(1)}, f32[512,512]{1,0:T(8,128)S(1)}, f32[512,256]{1,0:T(8,128)S(1)}, f32[512,256]{1,0:T(8,128)S(1)}) custom-call(s32[4]{0:T(128)S(1)} %pad_add_fusion.numbers_ref, bf16[512,512]{1,0:T(8,128)(2,1)S(1)} %collective-permute-done.7.refs_0_, ...), custom_call_target="tpu_custom_call", output_to_operand_aliasing={{0}: (5, {}), {1}: (6, {}), {2}: (7, {}), {3}: (8, {})} | custom-call | flops 1431655808 | bytes 8388608 | tf_op jit(solution)/shard_map/pallas_call | solution.py:94
  95.3 2.8 %shard_map.83 = (f32[512,512]{1,0:T(8,128)S(1)}, f32[512,512]{1,0:T(8,128)S(1)}, f32[512,256]{1,0:T(8,128)S(1)}, f32[512,256]{1,0:T(8,128)S(1)}) custom-call(s32[4]{0:T(128)S(1)} %pad_add_fusion.numbers_ref, bf16[512,512]{1,0:T(8,128)(2,1)S(1)} %collective-permute-done.7.refs_0_, ...), custom_call_target="tpu_custom_call", output_to_operand_aliasing={{0}: (4, {}), {1}: (5, {}), {2}: (6, {}), {3}: (7, {})} | custom-call | flops 715827904 | bytes 7864320 | tf_op jit(solution)/shard_map/pallas_call | solution.py:94
  98.2 0.9 shard_map.85
  99.1 4.5 %collective-permute-start.21 = (bf16[512,512]{1,0:T(8,128)(2,1)S(1)}, bf16[512,512]{1,0:T(8,128)(2,1)S(1)}, u32[]{:S(2)}, u32[]{:S(2)}) collective-permute-start(bf16[512,512]{1,0:T(8,128)(2,1)S(1)} %shard_map.85), channel_id=1, source_target_pairs={{0,0},{6,1},{2,2},{4,3},{1,4},{7,5},{3,6},{5,7},{8,8},{14,9},{10,1... | collective-permute-start | bytes 1572872 | tf_op jit(solution)/shard_map/ppermute | solution.py:462
  103.6 0.9 shard_map.84
  104.5 2.8 %collective-permute-start.19 = (bf16[512,512]{1,0:T(8,128)(2,1)S(1)}, bf16[512,512]{1,0:T(8,128)(2,1)S(1)}, u32[]{:S(2)}, u32[]{:S(2)}) collective-permute-start(bf16[512,512]{1,0:T(8,128)(2,1)S(1)} %shard_map.84), channel_id=1, source_target_pairs={{2,0},{4,1},{0,2},{6,3},{3,4},{5,5},{1,6},{7,7},{10,8},{12,9},{8,1... | collective-permute-start | bytes 1572872 | tf_op jit(solution)/shard_map/ppermute | solution.py:462
  107.3 8.7 %collective-permute-done.21.refs_0_ = bf16[512,512]{1,0:T(8,128)(2,1)S(1)} collective-permute-done((bf16[512,512]{1,0:T(8,128)(2,1)S(1)}, bf16[512,512]{1,0:T(8,128)(2,1)S(1)}, u32[]{:S(2)}, u32[]{:S(2)}) %collective-permute-start.21) | collective-permute-done | bytes 524320 | tf_op jit(solution)/shard_map/ppermute | solution.py:462
  116.0 2.4 %collective-permute-done.19.refs_0_ = bf16[512,512]{1,0:T(8,128)(2,1)S(1)} collective-permute-done((bf16[512,512]{1,0:T(8,128)(2,1)S(1)}, bf16[512,512]{1,0:T(8,128)(2,1)S(1)}, u32[]{:S(2)}, u32[]{:S(2)}) %collective-permute-start.19) | collective-permute-done | bytes 524320 | tf_op jit(solution)/shard_map/ppermute | solution.py:462
  118.4 2.6 %shard_map.86.refs_2_ = f32[512,1792]{1,0:T(8,128)S(1)} custom-call(s32[4]{0:T(128)S(1)} %pad_add_fusion.numbers_ref, bf16[512,512]{1,0:T(8,128)(2,1)S(1)} %collective-permute-done.21.refs_0_, bf16[512,512]{1,0:T(8,128)(2,1)S(1)} %collective-permute-done.22.refs_1_, bf16[1024,1792]{1,0:T(8,128)(2,1)S(1)} %get-tuple-element.66.refs_2_), custom_call_target="tpu_custom_call" | custom-call | flops 1879048192 | bytes 8388608 | tf_op jit(solution)/shard_map/pallas_call | solution.py:94
  121.0 1.8 %shard_map.87.refs_2_ = f32[512,1792]{1,0:T(8,128)S(1)} custom-call(s32[4]{0:T(128)S(1)} %pad_add_fusion.numbers_ref, bf16[512,512]{1,0:T(8,128)(2,1)S(1)} %collective-permute-done.19.refs_0_, bf16[1024,1792]{1,0:T(8,128)(2,1)S(1)} %get-tuple-element.63.refs_1_, f32[512,1792]{1,0:T(8,128)S(1)} %shard_map.86.refs_2_), custom_call_target="tpu_custom_call", output_to_operand_aliasing={{}: (3, {})} | custom-call | flops 939524096 | bytes 11534336 | tf_op jit(solution)/shard_map/pallas_call | solution.py:94
  122.9 0.0 copy-start.6
  122.9 2.3 %shard_map.88 = (f32[512,1792]{1,0:T(8,128)S(1)}, f32[512,128]{1,0:T(8,128)S(1)}) custom-call(s32[4]{0:T(128)S(1)} %pad_add_fusion.numbers_ref, bf16[512,512]{1,0:T(8,128)(2,1)S(1)} %collective-permute-done.20.refs_0_, bf16[1024,1792]{1,0:T(8,128)(2,1)S(1)} %get-tuple-element.63.refs_1_, ...), custom_call_target="tpu_custom_call", output_to_operand_aliasing={{0}: (3, {})} | custom-call | flops 939524096 | bytes 11796480 | tf_op jit(solution)/shard_map/pallas_call | solution.py:94
  125.2 0.6 collective-permute-start.23
  125.7 1.2 collective-permute-done.23.refs_1_
  126.9 2.4 %shard_map.89 = bf16[512,1792]{1,0:T(8,128)(2,1)} custom-call(bf16[512,1792]{1,0:T(8,128)(2,1)S(1)} %copy-done.3, f32[512,1792]{1,0:T(8,128)S(1)} %get-tuple-element.67.share, f32[14,128]{1,0:T(8,128)S(1)} %bitcast.13, f32[512,128]{1,0:T(8,128)S(1)} %get-tuple-element.68.refs_0_, f32[512,128]{1,0:T(8,128)S(1)} %collective-permute-done.23.refs_1_), custom_call_target="tpu_custom_call" | custom-call | flops 7340032 | bytes 7340032 | tf_op jit(solution)/shard_map/pallas_call | solution.py:298
  (29 shorter events, 0.1 us)
Async XLA Ops:
  0.0 7.6 %collective-permute-start = (bf16[512,1792]{1,0:T(8,128)(2,1)}, bf16[512,1792]{1,0:T(8,128)(2,1)S(1)}, u32[]{:S(2)}, u32[]{:S(2)}) collective-permute-start(bf16[512,1792]{1,0:T(8,128)(2,1)} %tokens.1), channel_id=1, source_target_pairs={{0,1},{1,0},{2,3},{3,2},{4,5},{5,4},{6,7},{7,6},{8,9},{9,8},{10,11... | collective-permute-start | bytes 5505032 | tf_op jit(solution)/shard_map/ppermute | solution.py:443
  1.8 10.9 %slice-start = ((s8[7340032]{0:T(1024)(128)(4,1)}), s8[4194304]{0:T(1024)(128)(4,1)S(1)}, s32[]{:S(2)}) async-start(s8[7340032]{0:T(1024)(128)(4,1)} %bitcast.6), calls=%async_computation | async-start | bytes 8388608
  1.8 1.7 %copy-start.2 = (bf16[512,1792]{1,0:T(8,128)(2,1)S(1)}, bf16[512,1792]{1,0:T(8,128)(2,1)}, u32[]{:S(2)}) copy-start(bf16[512,1792]{1,0:T(8,128)(2,1)} %tokens.1) | copy-start | bytes 5505028
  3.4 0.9 copy-start.4
  4.3 0.7 copy-start.5
  5.0 2.6 %copy-start = (bf16[3584,512]{1,0:T(8,128)(2,1)S(1)}, bf16[3584,512]{1,0:T(8,128)(2,1)}, u32[]{:S(2)}) copy-start(bf16[3584,512]{1,0:T(8,128)(2,1)} %refs_3_.4) | copy-start | bytes 11010052
  5.0 3.2 %copy-start.1 = (bf16[3584,512]{1,0:T(8,128)(2,1)S(1)}, bf16[3584,512]{1,0:T(8,128)(2,1)}, u32[]{:S(2)}) copy-start(bf16[3584,512]{1,0:T(8,128)(2,1)} %refs_4_.1) | copy-start | bytes 11010052
  5.0 3.7 %copy-start.3 = (bf16[512,1792]{1,0:T(8,128)(2,1)S(1)}, bf16[512,1792]{1,0:T(8,128)(2,1)}, u32[]{:S(2)}) copy-start(bf16[512,1792]{1,0:T(8,128)(2,1)} %tokens.1) | copy-start | bytes 5505028
  5.0 7.7 %slice-start.1 = ((s8[7340032]{0:T(1024)(128)(4,1)}), s8[3145728]{0:T(1024)(128)(4,1)S(1)}, s32[]{:S(2)}) async-start(s8[7340032]{0:T(1024)(128)(4,1)} %bitcast.6), calls=%async_computation.1 | async-start | bytes 6291456
  6.0 1.6 %collective-permute-start.1 = (f32[512,128]{1,0:T(8,128)S(1)}, f32[512,128]{1,0:T(8,128)S(1)}, u32[]{:S(2)}, u32[]{:S(2)}) collective-permute-start(f32[512,128]{1,0:T(8,128)S(1)} %shard_map.73.refs_2_), channel_id=1, source_target_pairs={{0,1},{1,0},{2,3},{3,2},{4,5},{5,4},{6,7},{7,6},{8,9},{9,8},{10,11... | collective-permute-start | bytes 786440 | tf_op jit(solution)/shard_map/ppermute | solution.py:443
  12.7 3.0 %slice-start.2 = ((s8[7340032]{0:T(1024)(128)(4,1)}), s8[4194304]{0:T(1024)(128)(4,1)S(1)}, s32[]{:S(2)}) async-start(s8[7340032]{0:T(1024)(128)(4,1)} %bitcast.8), calls=%async_computation.2 | async-start | bytes 8388608
  12.7 3.1 %slice-start.3 = ((s8[7340032]{0:T(1024)(128)(4,1)}), s8[3145728]{0:T(1024)(128)(4,1)S(1)}, s32[]{:S(2)}) async-start(s8[7340032]{0:T(1024)(128)(4,1)} %bitcast.8), calls=%async_computation.3 | async-start | bytes 6291456
  15.6 71.0 %collective-permute-start.18 = (bf16[1024,1792]{1,0:T(8,128)(2,1)S(1)}, bf16[1024,1792]{1,0:T(8,128)(2,1)S(1)}, u32[]{:S(2)}, u32[]{:S(2)}) collective-permute-start(bf16[1024,1792]{1,0:T(8,128)(2,1)S(1)} %get-tuple-element.48), channel_id=1, source_target_pairs={{0,1},{1,0},{2,3},{3,2},{4,5},{5,4},{6,7},{7,6},{8,9},{9,8},{10,11... | collective-permute-start | bytes 11010056 | tf_op jit(solution)/shard_map/ppermute | solution.py:443
  18.5 14.5 %collective-permute-start.7 = (bf16[512,512]{1,0:T(8,128)(2,1)S(1)}, bf16[512,512]{1,0:T(8,128)(2,1)S(1)}, u32[]{:S(2)}, u32[]{:S(2)}) collective-permute-start(bf16[512,512]{1,0:T(8,128)(2,1)S(1)} %shard_map.77), channel_id=1, source_target_pairs={{0,0},{1,6},{2,2},{3,4},{4,1},{5,7},{6,3},{7,5},{8,8},{9,14},{10,1... | collective-permute-start | bytes 1572872 | tf_op jit(solution)/shard_map/ppermute | solution.py:459
  22.8 15.8 %collective-permute-start.10 = (bf16[512,512]{1,0:T(8,128)(2,1)S(1)}, bf16[512,512]{1,0:T(8,128)(2,1)S(1)}, u32[]{:S(2)}, u32[]{:S(2)}) collective-permute-start(bf16[512,512]{1,0:T(8,128)(2,1)S(1)} %get-tuple-element.39), channel_id=1, source_target_pairs={{0,8},{2,10},{4,12},{6,14},{8,16},{10,18},{12,20},{14,22},{16,24},... | collective-permute-start | bytes 1572872 | tf_op jit(solution)/shard_map/ppermute | solution.py:446
  26.0 15.7 %collective-permute-start.16 = (bf16[512,512]{1,0:T(8,128)(2,1)S(1)}, bf16[512,512]{1,0:T(8,128)(2,1)S(1)}, u32[]{:S(2)}, u32[]{:S(2)}) collective-permute-start(bf16[512,512]{1,0:T(8,128)(2,1)S(1)} %get-tuple-element.39), channel_id=1, source_target_pairs={{0,0},{1,6},{2,2},{3,4},{4,1},{5,7},{6,3},{7,5},{8,8},{9,14},{10,1... | collective-permute-start | bytes 1572872 | tf_op jit(solution)/shard_map/ppermute | solution.py:459
  28.5 18.6 %collective-permute-start.3 = (bf16[512,512]{1,0:T(8,128)(2,1)S(1)}, bf16[512,512]{1,0:T(8,128)(2,1)S(1)}, u32[]{:S(2)}, u32[]{:S(2)}) collective-permute-start(bf16[512,512]{1,0:T(8,128)(2,1)S(1)} %get-tuple-element.38), channel_id=1, source_target_pairs={{0,8},{2,10},{4,12},{6,14},{8,16},{10,18},{12,20},{14,22},{16,24},... | collective-permute-start | bytes 1572872 | tf_op jit(solution)/shard_map/ppermute | solution.py:446
  33.1 18.8 %collective-permute-start.2 = (bf16[512,512]{1,0:T(8,128)(2,1)S(1)}, bf16[512,512]{1,0:T(8,128)(2,1)S(1)}, u32[]{:S(2)}, u32[]{:S(2)}) collective-permute-start(bf16[512,512]{1,0:T(8,128)(2,1)S(1)} %shard_map.75), channel_id=1, source_target_pairs={{0,2},{1,4},{2,0},{3,6},{4,3},{5,5},{6,1},{7,7},{8,10},{9,12},{10,... | collective-permute-start | bytes 1572872 | tf_op jit(solution)/shard_map/ppermute | solution.py:459
  38.7 23.4 %collective-permute-start.11 = (bf16[512,512]{1,0:T(8,128)(2,1)S(1)}, bf16[512,512]{1,0:T(8,128)(2,1)S(1)}, u32[]{:S(2)}, u32[]{:S(2)}) collective-permute-start(bf16[512,512]{1,0:T(8,128)(2,1)S(1)} %collective-permute-done.10), channel_id=1, source_target_pairs={{0,0},{1,6},{2,2},{3,4},{4,1},{5,7},{6,3},{7,5},{8,8},{9,14},{10,1... | collective-permute-start | bytes 1572872 | tf_op jit(solution)/shard_map/ppermute | solution.py:459
  41.7 22.3 %collective-permute-start.8 = (bf16[512,512]{1,0:T(8,128)(2,1)S(1)}, bf16[512,512]{1,0:T(8,128)(2,1)S(1)}, u32[]{:S(2)}, u32[]{:S(2)}) collective-permute-start(bf16[512,512]{1,0:T(8,128)(2,1)S(1)} %get-tuple-element.38), channel_id=1, source_target_pairs={{0,2},{1,4},{2,0},{3,6},{4,3},{5,5},{6,1},{7,7},{8,10},{9,12},{10,... | collective-permute-start | bytes 1572872 | tf_op jit(solution)/shard_map/ppermute | solution.py:459
  47.1 16.9 %collective-permute-start.4 = (bf16[512,512]{1,0:T(8,128)(2,1)S(1)}, bf16[512,512]{1,0:T(8,128)(2,1)S(1)}, u32[]{:S(2)}, u32[]{:S(2)}) collective-permute-start(bf16[512,512]{1,0:T(8,128)(2,1)S(1)} %collective-permute-done.3), channel_id=1, source_target_pairs={{0,2},{1,4},{2,0},{3,6},{4,3},{5,5},{6,1},{7,7},{8,10},{9,12},{10,... | collective-permute-start | bytes 1572872 | tf_op jit(solution)/shard_map/ppermute | solution.py:459
  51.9 14.1 %collective-permute-start.17 = (bf16[512,512]{1,0:T(8,128)(2,1)S(1)}, bf16[512,512]{1,0:T(8,128)(2,1)S(1)}, u32[]{:S(2)}, u32[]{:S(2)}) collective-permute-start(bf16[512,512]{1,0:T(8,128)(2,1)S(1)} %collective-permute-done.16.refs_2_), channel_id=1, source_target_pairs={{0,1},{1,0},{2,3},{3,2},{4,5},{5,4},{6,7},{7,6},{8,9},{9,8},{10,11... | collective-permute-start | bytes 1572872 | tf_op jit(solution)/shard_map/ppermute | solution.py:443
  62.0 12.9 %collective-permute-start.12 = (bf16[512,512]{1,0:T(8,128)(2,1)S(1)}, bf16[512,512]{1,0:T(8,128)(2,1)S(1)}, u32[]{:S(2)}, u32[]{:S(2)}) collective-permute-start(bf16[512,512]{1,0:T(8,128)(2,1)S(1)} %collective-permute-done.11.refs_2_), channel_id=1, source_target_pairs={{0,8},{2,10},{4,12},{6,14},{8,16},{10,18},{12,20},{14,22},{16,24},... | collective-permute-start | bytes 1572872 | tf_op jit(solution)/shard_map/ppermute | solution.py:446
  64.0 10.9 %collective-permute-start.15 = (bf16[512,512]{1,0:T(8,128)(2,1)S(1)}, bf16[512,512]{1,0:T(8,128)(2,1)S(1)}, u32[]{:S(2)}, u32[]{:S(2)}) collective-permute-start(bf16[512,512]{1,0:T(8,128)(2,1)S(1)} %collective-permute-done.11.refs_2_), channel_id=1, source_target_pairs={{0,1},{1,0},{2,3},{3,2},{4,5},{5,4},{6,7},{7,6},{8,9},{9,8},{10,11... | collective-permute-start | bytes 1572872 | tf_op jit(solution)/shard_map/ppermute | solution.py:443
  64.0 19.1 %collective-permute-start.5 = (bf16[512,512]{1,0:T(8,128)(2,1)S(1)}, bf16[512,512]{1,0:T(8,128)(2,1)S(1)}, u32[]{:S(2)}, u32[]{:S(2)}) collective-permute-start(bf16[512,512]{1,0:T(8,128)(2,1)S(1)} %collective-permute-done.4.refs_2_), channel_id=1, source_target_pairs={{0,8},{2,10},{4,12},{6,14},{8,16},{10,18},{12,20},{14,22},{16,24},... | collective-permute-start | bytes 1572872 | tf_op jit(solution)/shard_map/ppermute | solution.py:446
  66.0 20.6 %collective-permute-start.14 = (bf16[512,512]{1,0:T(8,128)(2,1)S(1)}, bf16[512,512]{1,0:T(8,128)(2,1)S(1)}, u32[]{:S(2)}, u32[]{:S(2)}) collective-permute-start(bf16[512,512]{1,0:T(8,128)(2,1)S(1)} %collective-permute-done.4.refs_2_), channel_id=1, source_target_pairs={{0,1},{1,0},{2,3},{3,2},{4,5},{5,4},{6,7},{7,6},{8,9},{9,8},{10,11... | collective-permute-start | bytes 1572872 | tf_op jit(solution)/shard_map/ppermute | solution.py:443
  74.9 15.6 %collective-permute-start.13 = (bf16[512,512]{1,0:T(8,128)(2,1)S(1)}, bf16[512,512]{1,0:T(8,128)(2,1)S(1)}, u32[]{:S(2)}, u32[]{:S(2)}) collective-permute-start(bf16[512,512]{1,0:T(8,128)(2,1)S(1)} %collective-permute-done.12.refs_2_), channel_id=1, source_target_pairs={{0,1},{1,0},{2,3},{3,2},{4,5},{5,4},{6,7},{7,6},{8,9},{9,8},{10,11... | collective-permute-start | bytes 1572872 | tf_op jit(solution)/shard_map/ppermute | solution.py:443
  74.9 17.3 %collective-permute-start.9 = (bf16[512,512]{1,0:T(8,128)(2,1)S(1)}, bf16[512,512]{1,0:T(8,128)(2,1)S(1)}, u32[]{:S(2)}, u32[]{:S(2)}) collective-permute-start(bf16[512,512]{1,0:T(8,128)(2,1)S(1)} %collective-permute-done.8.refs_2_), channel_id=1, source_target_pairs={{0,1},{1,0},{2,3},{3,2},{4,5},{5,4},{6,7},{7,6},{8,9},{9,8},{10,11... | collective-permute-start | bytes 1572872 | tf_op jit(solution)/shard_map/ppermute | solution.py:443
  83.2 15.0 %collective-permute-start.6 = (bf16[512,512]{1,0:T(8,128)(2,1)S(1)}, bf16[512,512]{1,0:T(8,128)(2,1)S(1)}, u32[]{:S(2)}, u32[]{:S(2)}) collective-permute-start(bf16[512,512]{1,0:T(8,128)(2,1)S(1)} %collective-permute-done.5.refs_2_), channel_id=1, source_target_pairs={{0,1},{1,0},{2,3},{3,2},{4,5},{5,4},{6,7},{7,6},{8,9},{9,8},{10,11... | collective-permute-start | bytes 1572872 | tf_op jit(solution)/shard_map/ppermute | solution.py:443
  99.1 16.9 %collective-permute-start.21 = (bf16[512,512]{1,0:T(8,128)(2,1)S(1)}, bf16[512,512]{1,0:T(8,128)(2,1)S(1)}, u32[]{:S(2)}, u32[]{:S(2)}) collective-permute-start(bf16[512,512]{1,0:T(8,128)(2,1)S(1)} %shard_map.85), channel_id=1, source_target_pairs={{0,0},{6,1},{2,2},{4,3},{1,4},{7,5},{3,6},{5,7},{8,8},{14,9},{10,1... | collective-permute-start | bytes 1572872 | tf_op jit(solution)/shard_map/ppermute | solution.py:462
  104.5 13.9 %collective-permute-start.19 = (bf16[512,512]{1,0:T(8,128)(2,1)S(1)}, bf16[512,512]{1,0:T(8,128)(2,1)S(1)}, u32[]{:S(2)}, u32[]{:S(2)}) collective-permute-start(bf16[512,512]{1,0:T(8,128)(2,1)S(1)} %shard_map.84), channel_id=1, source_target_pairs={{2,0},{4,1},{0,2},{6,3},{3,4},{5,5},{1,6},{7,7},{10,8},{12,9},{8,1... | collective-permute-start | bytes 1572872 | tf_op jit(solution)/shard_map/ppermute | solution.py:462
  116.0 2.4 %collective-permute-start.22 = (bf16[512,512]{1,0:T(8,128)(2,1)S(1)}, bf16[512,512]{1,0:T(8,128)(2,1)S(1)}, u32[]{:S(2)}, u32[]{:S(2)}) collective-permute-start(bf16[512,512]{1,0:T(8,128)(2,1)S(1)} %collective-permute-done.21.refs_0_), channel_id=1, source_target_pairs={{0,1},{1,0},{2,3},{3,2},{4,5},{5,4},{6,7},{7,6},{8,9},{9,8},{10,11... | collective-permute-start | bytes 1572872 | tf_op jit(solution)/shard_map/ppermute | solution.py:443
  118.4 4.5 %collective-permute-start.20 = (bf16[512,512]{1,0:T(8,128)(2,1)S(1)}, bf16[512,512]{1,0:T(8,128)(2,1)S(1)}, u32[]{:S(2)}, u32[]{:S(2)}) collective-permute-start(bf16[512,512]{1,0:T(8,128)(2,1)S(1)} %collective-permute-done.19.refs_0_), channel_id=1, source_target_pairs={{0,1},{1,0},{2,3},{3,2},{4,5},{5,4},{6,7},{7,6},{8,9},{9,8},{10,11... | collective-permute-start | bytes 1572872 | tf_op jit(solution)/shard_map/ppermute | solution.py:443
  122.9 4.0 %copy-start.6 = (f32[1792]{0:T(1024)S(1)}, f32[1792]{0:T(1024)}, u32[]{:S(2)}) copy-start(f32[1792]{0:T(1024)} %param.13) | copy-start | bytes 21508
  125.2 1.7 %collective-permute-start.23 = (f32[512,128]{1,0:T(8,128)S(1)}, f32[512,128]{1,0:T(8,128)S(1)}, u32[]{:S(2)}, u32[]{:S(2)}) collective-permute-start(f32[512,128]{1,0:T(8,128)S(1)} %get-tuple-element.68.refs_0_), channel_id=1, source_target_pairs={{0,1},{1,0},{2,3},{3,2},{4,5},{5,4},{6,7},{7,6},{8,9},{9,8},{10,11... | collective-permute-start | bytes 786440 | tf_op jit(solution)/shard_map/ppermute | solution.py:443

commit v2 on v1

--- a/solution.py
+++ b/solution.py
@@ -229,7 +229,7 @@
     return kernel_call(body, fetch, numbers, [normed, *tables, *weights], out, [], 8, flops)
 
 
-def out_projection(numbers, lefts, weight, some, total, last):
+def out_projection(numbers, lefts, weight, total, last):
     n = len(lefts)
     rows, width = lefts[0].shape
     out_width = weight.shape[1]
@@ -243,7 +243,7 @@
             left[:, k * width : (k + 1) * width] = inputs[k][...]
         for column in range(0, out_width, columns):
             here = slice(column, column + columns)
-            value = dot(left[...], weight_ref[some[0] * width : (some[-1] + 1) * width, here])
+            value = dot(left[...], weight_ref[:, here])
             if total is not None:
                 value = value + inputs[n + 1][:, here]
             outputs[0][:, here] = value
@@ -264,44 +264,53 @@
     return kernel_call(body, NOTHING, numbers, operands, out, scratch, 8, flops, aliases)
 
 
-def finish_kernel(n, tokens, share, gain, *refs):
-    square_refs, out, scale_ref = refs[:n], refs[n], refs[n + 1]
-    block, part = out.shape
+def finish_kernel(n, pieces, tokens, share, gain, *refs):
+    square_refs, out, held, scale_ref, copied = refs[:n], *refs[n:]
+    rows, part = held.shape
     lanes = scale_ref.shape[1]
-    base = pl.program_id(0) * block
-    at = pl.ds(pl.multiple_of(base, block), block)
-    total = square_refs[0][at, :]
+    total = square_refs[0][...]
     for ref in square_refs[1:]:
-        total = total + ref[at, :]
+        total = total + ref[...]
     total = jnp.sum(total, axis=-1, keepdims=True)
     scale = lax.rsqrt(total / (part * n) + norm_epsilon)
     scale_ref[...] = jnp.broadcast_to(scale, scale_ref.shape)
+    block = rows // pieces
     step = min(16, block)
 
     def some_rows(t, carry):
-        here = pl.ds(pl.multiple_of(t * step, step), step)
-        at = pl.ds(pl.multiple_of(base + t * step, step), step)
-        scale = scale_ref[here, :]
+        at = pl.ds(pl.multiple_of(t * step, step), step)
+        scale = scale_ref[at, :]
         for column in range(0, part, lanes):
             columns = slice(column, column + lanes)
             value = gain[column // lanes : column // lanes + 1, :] * share[at, columns] * scale
             value = tokens[at, columns].astype(jnp.float32) + value
-            out[here, columns] = value.astype(jnp.bfloat16)
+            held[at, columns] = value.astype(jnp.bfloat16)
         return carry
 
-    lax.fori_loop(0, block // step, some_rows, 0, unroll=2)
+    copies = []
+    for k in range(pieces):
+        steps = block // step
+        lax.fori_loop(k * steps, (k + 1) * steps, some_rows, 0, unroll=2)
+        at = slice(k * block, (k + 1) * block)
+        copies.append(pltpu.make_async_copy(held.at[at, :], out.at[at, :], copied.at[k]))
+        copies[-1].start()
+    for copy in copies:
+        copy.wait()
 
 
 def finish(tokens, share, gain, squares):
     rows, part = tokens.shape
-    step = min(128, rows)
+    pieces = 4 if rows % 64 == 0 else 1
     return pl.pallas_call(
-        functools.partial(finish_kernel, len(squares)),
-        grid=(rows // step,),
+        functools.partial(finish_kernel, len(squares), pieces),
         out_shape=jax.ShapeDtypeStruct((rows, part), jnp.bfloat16),
         in_specs=[VMEM] * (3 + len(squares)),
-        out_specs=pl.BlockSpec((step, part), lambda t: (t, 0)),
-        scratch_shapes=[pltpu.VMEM((step, min(128, part)), jnp.float32)],
+        out_specs=FAR,
+        scratch_shapes=[
+            pltpu.VMEM((rows, part), jnp.bfloat16),
+            pltpu.VMEM((rows, min(128, part)), jnp.float32),
+            pltpu.SemaphoreType.DMA((pieces,)),
+        ],
         compiler_params=pltpu.CompilerParams(vmem_limit_bytes=8 * MIB),
         cost_estimate=pl.CostEstimate(
             flops=8 * rows * part, bytes_accessed=8 * rows * part, transcendentals=0
@@ -322,16 +331,14 @@
     def body(scalars, inputs, outputs, scratch):
         q_refs, kv_refs = inputs[:n_q], inputs[n_q : n_q + n_kv]
         kv_all, key_numbers = scratch[:2]
-        state = scratch[2:] if last else outputs
+        state = outputs[n_q:] if last else outputs
         acc, den = state[:n_q], state[n_q:]
         for k in range(n_kv):
             kv_all[k * rows : (k + 1) * rows, :] = kv_refs[k][...]
             key_numbers[k] = key_blocks[k](scalars)
-        for k, ref in enumerate(state):
+        for ref in state:
             if first:
                 ref[...] = jnp.zeros_like(ref)
-            elif last:
-                ref[...] = inputs[n_q + n_kv + k][...]
 
         def add(r, keys_at, delta):
             for head in range(heads):
@@ -415,11 +422,10 @@
     operands = [*queries, *pieces] + ([] if first else list(totals))
     aliases = {}
     out = [jax.ShapeDtypeStruct(shape, jnp.float32) for shape in shapes]
-    if last:
-        scratch += [pltpu.VMEM(shape, jnp.float32) for shape in shapes]
-        out = [jax.ShapeDtypeStruct((rows, width), jnp.bfloat16)] * n_q
-    elif not first:
-        aliases = {n_q + n_kv + k: k for k in range(2 * n_q)}
+    n_attended = n_q if last else 0
+    out = [jax.ShapeDtypeStruct((rows, width), jnp.bfloat16)] * n_attended + out
+    if not first:
+        aliases = {n_q + n_kv + k: n_attended + k for k in range(2 * n_q)}
     flops = n_q * n_kv * heads * 4 * rows * rows * HD * 2 // 3
     return kernel_call(body, fetch, numbers, operands, out, scratch, 14, flops, aliases)
 
@@ -479,7 +485,7 @@
     tables = rope_tables(positions, HD)
     lanes = min(128, part)
     gain_in, gain_out = pre_gain.reshape(-1, lanes), post_gain.reshape(-1, lanes)
-    (own_squares,) = sum_squares(numbers, tokens, [*tables, gain_in, gain_out], NOTHING)
+    (own_squares,) = sum_squares(numbers, tokens, [*tables], NOTHING)
     kv_weights = [key_weight, value_weight]
     squares = [own_squares] + [over_cores(own_squares, by) for by in others]
     kv_blocks = [
@@ -549,26 +555,25 @@
         return merged[lag, turn, by]
 
     out_fetch = []
-    for turn in turns:
+    for by in range(cores):
         blocks = []
-        for by in range(cores):
+        for turn in turns:
             blocks.append(
                 (
                     by,
-                    by * piece_width,
+                    turn * piece_width,
                     0,
                     (piece_width, part),
                     held_by(by, turn, piece_width),
                     None if by else (lambda ref: ref[0] * part),
                 )
             )
-        out_fetch.append(((piece_width * cores, part), blocks))
+        out_fetch.append(((piece_width * kv_heads, part), blocks))
     calls = [[(0, 0, by) for by in range(cores)]]
     for lag in range(1, hops + 1):
         for turn in turns:
             calls.append([(lag, turn, by) for by in range(cores)])
     calls[-1:-1] = [[(0, turn, by) for by in range(cores)] for turn in turns[1:]]
-    calls[-1:] = [calls[-1][:1], calls[-1][1:]]
     n_q = len(q_pieces)
     totals, attended, out_blocks = None, [], None
 
@@ -589,26 +594,25 @@
         )
 
     for index, call in enumerate(calls[:-1]):
-        fetch = Fetch(row_blocks, out_fetch) if index == len(calls) - 5 else NOTHING
+        fetch = Fetch(row_blocks, out_fetch) if index == len(calls) - 4 else NOTHING
         totals = run(call, range(n_q), totals, False, fetch)
         if fetch is not NOTHING:
             totals, out_blocks = totals[: 2 * n_q], totals[2 * n_q :]
     for r in range(n_q):
         state = [totals[r], totals[n_q + r]]
-        attended += run(calls[-1], [r], state, True, NOTHING)
+        call = calls[-1]
+        if r == 0:
+            state = run(call[:1], [r], state, False, NOTHING)
+            call = call[1:]
+        attended += run(call, [r], state, True, NOTHING)[:1]
     total = None
-    for turn, o in enumerate(attended):
-        own = gather_back(o, turn)
-        lefts = [own] + [over_cores(own, by) for by in others]
-        parts = [range(cores)]
-        if turn == kv_heads - 1:
-            parts = [range(1), range(1, cores)]
-        for index, some in enumerate(parts):
-            last = turn == kv_heads - 1 and index == len(parts) - 1
-            out = out_projection(
-                numbers, [lefts[k] for k in some], out_blocks[turn], some, total, last
-            )
-            total = out[0]
+    back = [gather_back(o, turn) for turn, o in enumerate(attended)]
+    for by in range(cores):
+        lefts = back
+        if by:
+            lefts = [over_cores(own, by) for own in back]
+        out = out_projection(numbers, lefts, out_blocks[by], total, by == cores - 1)
+        total = out[0]
     share, own_squares = out
     squares = [own_squares] + [over_cores(own_squares, by) for by in others]
     return finish(tokens, share, gain_out, squares)

time: 131 us -> 126 us (0.962)
  waiting for transfers between devices: 40.9 us -> 29.9 us
  starting transfers between devices: 39.2 us -> 48.3 us
  Pallas kernels: 43.4 us -> 41.3 us
  local copies, waits for them, and re-layouts: 4.4 us -> 2.69 us
    ppermute x12, starting transfers between devices: 2.65 us -> 11.3 us  [over_cores(): lax.ppermute(value, 'head', [(c, (c + by) % cores) for c in range(cores)])]
    ppermute x2, waiting for transfers between devices: 11.1 us -> 4.01 us  [gather_back(): lax.ppermute(value, ('seq', 'head'), [(b, a) for a, b in route(turn)])]
    ppermute x4, starting transfers between devices: 8.96 us -> 11.2 us  [next_plane(): lax.ppermute(value, 'seq', [(i, i + plane) for i in range(n_seq - plane)])]
    ppermute x4, waiting for transfers between devices: 17.1 us -> 15.1 us  [next_plane(): lax.ppermute(value, 'seq', [(i, i + plane) for i in range(n_seq - plane)])]
    ppermute x6, waiting for transfers between devices: 10.1 us -> 8.16 us  [spread(): return lax.ppermute(value, ('seq', 'head'), route(turn))]
    ppermute x6, starting transfers between devices: 20.2 us -> 18.5 us  [spread(): return lax.ppermute(value, ('seq', 'head'), route(turn))]
    unnamed x22 -> x18, local copies, waits for them, and re-layouts: 4.4 us -> 2.69 us
    pallas_call x16 -> x15, Pallas kernels: 40.9 us -> 39.5 us  [kernel_call(): pl.pallas_call(kernel, out_shape=list(out_shape) + fetch.shapes(), in_spe...]
  transfers between devices with their start and end apart: 24 -> 24, of which waited for: 9 -> 9; matrix products, arithmetic and copies ran while one was open for 1% -> 1% of each run, Pallas kernels for 24% -> 22%
where the time goes in v2:
time: 126 us; the launch traced here: 124 us
  starting transfers between devices  48.3 us (38%)
  Pallas kernels  41.3 us (33%)
  waiting for transfers between devices  29.9 us (24%)
  local copies, waits for them, and re-layouts  2.69 us (2%)
    pallas_call x15, Pallas kernels, kernel_call(): pl.pallas_call(kernel, out_shape=list(out_shape) + fetch.shapes(), in_spe...  39.5 us
    ppermute x6, starting transfers between devices, spread(): return lax.ppermute(value, ('seq', 'head'), route(turn))  18.5 us
    ppermute x4, waiting for transfers between devices, next_plane(): lax.ppermute(value, 'seq', [(i, i + plane) for i in range(n_seq - plane)])  15.1 us
    ppermute x12, starting transfers between devices, over_cores(): lax.ppermute(value, 'head', [(c, (c + by) % cores) for c in range(cores)])  11.3 us
    ppermute x4, starting transfers between devices, next_plane(): lax.ppermute(value, 'seq', [(i, i + plane) for i in range(n_seq - plane)])  11.2 us
    ppermute x6, waiting for transfers between devices, spread(): return lax.ppermute(value, ('seq', 'head'), route(turn))  8.16 us
    ppermute x2, starting transfers between devices, gather_back(): lax.ppermute(value, ('seq', 'head'), [(b, a) for a, b in route(turn)])  7.32 us
    ppermute x2, waiting for transfers between devices, gather_back(): lax.ppermute(value, ('seq', 'head'), [(b, a) for a, b in route(turn)])  4.01 us
  transfers between devices with their start and end apart: 24, of which 9 were waited for; matrix products, arithmetic and copies ran while one was open for 1% of the time, Pallas kernels for 22%

profile of v2, /device:TPU:17, one launch (start us, length us, event | category | flops | bytes accessed | tf_op | source)
XLA Modules:
  0.0 123.9 jit_solution(101596487009130418)
XLA Ops:
  0.0 0.7 collective-permute-start
  0.7 1.0 multiply_sine_fusion
  1.7 0.1 pad_add_fusion.numbers_ref
  1.8 1.5 %copy-done.3 = bf16[512,1792]{1,0:T(8,128)(2,1)S(1)} copy-done((bf16[512,1792]{1,0:T(8,128)(2,1)S(1)}, bf16[512,1792]{1,0:T(8,128)(2,1)}, u32[]{:S(2)}) %copy-start.3) | copy-done | bytes 1835032
  3.3 1.0 shard_map.73.refs_2_
  4.3 0.1 collective-permute-start.1
  4.4 1.5 %collective-permute-done.1.refs_3_ = f32[512,128]{1,0:T(8,128)S(1)} collective-permute-done((f32[512,128]{1,0:T(8,128)S(1)}, f32[512,128]{1,0:T(8,128)S(1)}, u32[]{:S(2)}, u32[]{:S(2)}) %collective-permute-start.1) | collective-permute-done | bytes 262176 | tf_op jit(solution)/shard_map/ppermute | solution.py:449
  5.9 0.0 collective-permute-done.refs_1_
  5.9 0.5 copy-done.2
  6.4 0.5 copy-done.4
  6.9 4.0 %shard_map.74 = (bf16[512,3584]{1,0:T(8,128)(2,1)S(1)}, bf16[512,512]{1,0:T(8,128)(2,1)S(1)}) custom-call(s32[4]{0:T(128)S(1)} %pad_add_fusion.numbers_ref, bf16[512,1792]{1,0:T(8,128)(2,1)S(1)} %copy-done.4, bf16[512,1792]{1,0:T(8,128)(2,1)S(1)} %collective-permute-done.refs_1_, f32[512,128]{1,0:T(8,128)S(1)} %shard_map.73.refs_2_, ...), custom_call_target="tpu_custom_call" | custom-call | flops 1879048192 | bytes 16267264 | tf_op jit(solution)/shard_map/pallas_call | solution.py:94
  11.0 0.0 slice-start
  11.0 0.0 slice-start.1
  11.0 2.9 %shard_map.76 = (bf16[512,512]{1,0:T(8,128)(2,1)S(1)}, bf16[1024,1792]{1,0:T(8,128)(2,1)S(1)}) custom-call(s32[4]{0:T(128)S(1)} %pad_add_fusion.numbers_ref, bf16[512,3584]{1,0:T(8,128)(2,1)S(1)} %get-tuple-element.37.refs_0_, f32[512,128]{1,0:T(8,128)S(1)} %get-tuple-element.70.refs_1_.refs_5_, f32[512,128]{1,0:T(8,128)S(1)} %get-tuple-element.69.refs_2_.refs_6_, ...), custom_call_target="tpu_custom_call" | custom-call | flops 1879048192 | bytes 12058624 | tf_op jit(solution)/shard_map/pallas_call | solution.py:94
  13.9 0.1 collective-permute-start.18
  14.0 0.2 slice-done.1
  14.2 2.6 %shard_map.77 = bf16[512,512]{1,0:T(8,128)(2,1)S(1)} custom-call(s32[4]{0:T(128)S(1)} %pad_add_fusion.numbers_ref, bf16[512,3584]{1,0:T(8,128)(2,1)S(1)} %get-tuple-element.37.refs_0_, f32[512,128]{1,0:T(8,128)S(1)} %get-tuple-element.70.refs_1_.refs_5_, f32[512,128]{1,0:T(8,128)S(1)} %get-tuple-element.69.refs_2_.refs_6_, bf16[3584,1024]{1,0:T(8,128)(2,1)S(1)} %bitcast.7), custom_call_target="tpu_custom_call" | custom-call | flops 1879048192 | bytes 12058624 | tf_op jit(solution)/shard_map/pallas_call | solution.py:94
  16.8 3.4 %collective-permute-start.7 = (bf16[512,512]{1,0:T(8,128)(2,1)S(1)}, bf16[512,512]{1,0:T(8,128)(2,1)S(1)}, u32[]{:S(2)}, u32[]{:S(2)}) collective-permute-start(bf16[512,512]{1,0:T(8,128)(2,1)S(1)} %shard_map.77), channel_id=1, source_target_pairs={{0,2},{1,4},{2,0},{3,6},{4,3},{5,5},{6,1},{7,7},{8,10},{9,12},{10,... | collective-permute-start | bytes 1572872 | tf_op jit(solution)/shard_map/ppermute | solution.py:465
  20.2 3.2 %collective-permute-start.10 = (bf16[512,512]{1,0:T(8,128)(2,1)S(1)}, bf16[512,512]{1,0:T(8,128)(2,1)S(1)}, u32[]{:S(2)}, u32[]{:S(2)}) collective-permute-start(bf16[512,512]{1,0:T(8,128)(2,1)S(1)} %get-tuple-element.39), channel_id=1, source_target_pairs={{0,8},{2,10},{4,12},{6,14},{8,16},{10,18},{12,20},{14,22},{16,24},... | collective-permute-start | bytes 1572872 | tf_op jit(solution)/shard_map/ppermute | solution.py:452
  23.4 3.4 %collective-permute-start.16 = (bf16[512,512]{1,0:T(8,128)(2,1)S(1)}, bf16[512,512]{1,0:T(8,128)(2,1)S(1)}, u32[]{:S(2)}, u32[]{:S(2)}) collective-permute-start(bf16[512,512]{1,0:T(8,128)(2,1)S(1)} %get-tuple-element.39), channel_id=1, source_target_pairs={{0,0},{1,6},{2,2},{3,4},{4,1},{5,7},{6,3},{7,5},{8,8},{9,14},{10,1... | collective-permute-start | bytes 1572872 | tf_op jit(solution)/shard_map/ppermute | solution.py:465
  26.8 1.9 %collective-permute-start.3 = (bf16[512,512]{1,0:T(8,128)(2,1)S(1)}, bf16[512,512]{1,0:T(8,128)(2,1)S(1)}, u32[]{:S(2)}, u32[]{:S(2)}) collective-permute-start(bf16[512,512]{1,0:T(8,128)(2,1)S(1)} %get-tuple-element.38), channel_id=1, source_target_pairs={{0,8},{2,10},{4,12},{6,14},{8,16},{10,18},{12,20},{14,22},{16,24},... | collective-permute-start | bytes 1572872 | tf_op jit(solution)/shard_map/ppermute | solution.py:452
  28.7 2.6 %shard_map.75 = bf16[512,512]{1,0:T(8,128)(2,1)S(1)} custom-call(s32[4]{0:T(128)S(1)} %pad_add_fusion.numbers_ref, bf16[512,3584]{1,0:T(8,128)(2,1)S(1)} %get-tuple-element.37.refs_0_, f32[512,128]{1,0:T(8,128)S(1)} %get-tuple-element.70.refs_1_.refs_5_, f32[512,128]{1,0:T(8,128)S(1)} %get-tuple-element.69.refs_2_.refs_6_, bf16[3584,1024]{1,0:T(8,128)(2,1)S(1)} %bitcast.7), custom_call_target="tpu_custom_call" | custom-call | flops 1879048192 | bytes 12058624 | tf_op jit(solution)/shard_map/pallas_call | solution.py:94
  31.3 0.0 collective-permute-done.7.refs_1_.refs_0_
  31.3 3.1 %collective-permute-start.2 = (bf16[512,512]{1,0:T(8,128)(2,1)S(1)}, bf16[512,512]{1,0:T(8,128)(2,1)S(1)}, u32[]{:S(2)}, u32[]{:S(2)}) collective-permute-start(bf16[512,512]{1,0:T(8,128)(2,1)S(1)} %shard_map.75), channel_id=1, source_target_pairs={{0,0},{1,6},{2,2},{3,4},{4,1},{5,7},{6,3},{7,5},{8,8},{9,14},{10,1... | collective-permute-start | bytes 1572872 | tf_op jit(solution)/shard_map/ppermute | solution.py:465
  34.4 0.7 collective-permute-done.10
  35.2 4.8 %collective-permute-start.11 = (bf16[512,512]{1,0:T(8,128)(2,1)S(1)}, bf16[512,512]{1,0:T(8,128)(2,1)S(1)}, u32[]{:S(2)}, u32[]{:S(2)}) collective-permute-start(bf16[512,512]{1,0:T(8,128)(2,1)S(1)} %collective-permute-done.10), channel_id=1, source_target_pairs={{0,0},{1,6},{2,2},{3,4},{4,1},{5,7},{6,3},{7,5},{8,8},{9,14},{10,1... | collective-permute-start | bytes 1572872 | tf_op jit(solution)/shard_map/ppermute | solution.py:465
  39.9 0.0 collective-permute-done.16.refs_2_
  40.0 1.9 %collective-permute-start.8 = (bf16[512,512]{1,0:T(8,128)(2,1)S(1)}, bf16[512,512]{1,0:T(8,128)(2,1)S(1)}, u32[]{:S(2)}, u32[]{:S(2)}) collective-permute-start(bf16[512,512]{1,0:T(8,128)(2,1)S(1)} %get-tuple-element.38), channel_id=1, source_target_pairs={{0,2},{1,4},{2,0},{3,6},{4,3},{5,5},{6,1},{7,7},{8,10},{9,12},{10,... | collective-permute-start | bytes 1572872 | tf_op jit(solution)/shard_map/ppermute | solution.py:465
  41.9 4.5 %collective-permute-done.3 = bf16[512,512]{1,0:T(8,128)(2,1)S(1)} collective-permute-done((bf16[512,512]{1,0:T(8,128)(2,1)S(1)}, bf16[512,512]{1,0:T(8,128)(2,1)S(1)}, u32[]{:S(2)}, u32[]{:S(2)}) %collective-permute-start.3) | collective-permute-done | bytes 524320 | tf_op jit(solution)/shard_map/ppermute | solution.py:452
  46.4 1.9 %collective-permute-start.4 = (bf16[512,512]{1,0:T(8,128)(2,1)S(1)}, bf16[512,512]{1,0:T(8,128)(2,1)S(1)}, u32[]{:S(2)}, u32[]{:S(2)}) collective-permute-start(bf16[512,512]{1,0:T(8,128)(2,1)S(1)} %collective-permute-done.3), channel_id=1, source_target_pairs={{0,2},{1,4},{2,0},{3,6},{4,3},{5,5},{6,1},{7,7},{8,10},{9,12},{10,... | collective-permute-start | bytes 1572872 | tf_op jit(solution)/shard_map/ppermute | solution.py:465
  48.3 2.5 %collective-permute-start.17 = (bf16[512,512]{1,0:T(8,128)(2,1)S(1)}, bf16[512,512]{1,0:T(8,128)(2,1)S(1)}, u32[]{:S(2)}, u32[]{:S(2)}) collective-permute-start(bf16[512,512]{1,0:T(8,128)(2,1)S(1)} %collective-permute-done.16.refs_2_), channel_id=1, source_target_pairs={{0,1},{1,0},{2,3},{3,2},{4,5},{5,4},{6,7},{7,6},{8,9},{9,8},{10,11... | collective-permute-start | bytes 1572872 | tf_op jit(solution)/shard_map/ppermute | solution.py:449
  50.8 8.2 %collective-permute-done.11.refs_2_ = bf16[512,512]{1,0:T(8,128)(2,1)S(1)} collective-permute-done((bf16[512,512]{1,0:T(8,128)(2,1)S(1)}, bf16[512,512]{1,0:T(8,128)(2,1)S(1)}, u32[]{:S(2)}, u32[]{:S(2)}) %collective-permute-start.11) | collective-permute-done | bytes 524320 | tf_op jit(solution)/shard_map/ppermute | solution.py:465
  59.0 4.2 %collective-permute-start.12 = (bf16[512,512]{1,0:T(8,128)(2,1)S(1)}, bf16[512,512]{1,0:T(8,128)(2,1)S(1)}, u32[]{:S(2)}, u32[]{:S(2)}) collective-permute-start(bf16[512,512]{1,0:T(8,128)(2,1)S(1)} %collective-permute-done.11.refs_2_), channel_id=1, source_target_pairs={{0,8},{2,10},{4,12},{6,14},{8,16},{10,18},{12,20},{14,22},{16,24},... | collective-permute-start | bytes 1572872 | tf_op jit(solution)/shard_map/ppermute | solution.py:452
  63.2 0.0 collective-permute-done.8.refs_2_
  63.2 0.1 collective-permute-start.15
  63.3 1.9 %collective-permute-start.5 = (bf16[512,512]{1,0:T(8,128)(2,1)S(1)}, bf16[512,512]{1,0:T(8,128)(2,1)S(1)}, u32[]{:S(2)}, u32[]{:S(2)}) collective-permute-start(bf16[512,512]{1,0:T(8,128)(2,1)S(1)} %collective-permute-done.4.refs_2_), channel_id=1, source_target_pairs={{0,8},{2,10},{4,12},{6,14},{8,16},{10,18},{12,20},{14,22},{16,24},... | collective-permute-start | bytes 1572872 | tf_op jit(solution)/shard_map/ppermute | solution.py:452
  65.2 0.0 collective-permute-done.17.refs_3_
  65.2 0.5 collective-permute-start.14
  65.7 6.5 %collective-permute-done.12.refs_2_ = bf16[512,512]{1,0:T(8,128)(2,1)S(1)} collective-permute-done((bf16[512,512]{1,0:T(8,128)(2,1)S(1)}, bf16[512,512]{1,0:T(8,128)(2,1)S(1)}, u32[]{:S(2)}, u32[]{:S(2)}) %collective-permute-start.12) | collective-permute-done | bytes 524320 | tf_op jit(solution)/shard_map/ppermute | solution.py:452
  72.2 0.0 collective-permute-start.13
  72.2 0.0 collective-permute-done.15.refs_3_
  72.2 0.5 collective-permute-start.9
  72.7 4.4 %shard_map.78 = (f32[512,512]{1,0:T(8,128)S(1)}, f32[512,512]{1,0:T(8,128)S(1)}, f32[512,256]{1,0:T(8,128)S(1)}, f32[512,256]{1,0:T(8,128)S(1)}) custom-call(s32[4]{0:T(128)S(1)} %pad_add_fusion.numbers_ref, bf16[512,512]{1,0:T(8,128)(2,1)S(1)} %collective-permute-done.2.refs_0_, bf16[512,512]{1,0:T(8,128)(2,1)S(1)} %collective-permute-done.7.refs_1_.refs_0_, ...), custom_call_target="tpu_custom_call" | custom-call | flops 1431655808 | bytes 5242880 | tf_op jit(solution)/shard_map/pallas_call | solution.py:94
  77.1 3.4 %collective-permute-done.5.refs_1_ = bf16[512,512]{1,0:T(8,128)(2,1)S(1)} collective-permute-done((bf16[512,512]{1,0:T(8,128)(2,1)S(1)}, bf16[512,512]{1,0:T(8,128)(2,1)S(1)}, u32[]{:S(2)}, u32[]{:S(2)}) %collective-permute-start.5) | collective-permute-done | bytes 524320 | tf_op jit(solution)/shard_map/ppermute | solution.py:452
  80.5 3.4 %shard_map.79 = (f32[512,512]{1,0:T(8,128)S(1)}, f32[512,512]{1,0:T(8,128)S(1)}, f32[512,256]{1,0:T(8,128)S(1)}, f32[512,256]{1,0:T(8,128)S(1)}) custom-call(s32[4]{0:T(128)S(1)} %pad_add_fusion.numbers_ref, bf16[512,512]{1,0:T(8,128)(2,1)S(1)} %collective-permute-done.2.refs_0_, ...), custom_call_target="tpu_custom_call", output_to_operand_aliasing={{0}: (5, {}), {1}: (6, {}), {2}: (7, {}), {3}: (8, {})} | custom-call | flops 1431655808 | bytes 8388608 | tf_op jit(solution)/shard_map/pallas_call | solution.py:94
  83.9 0.0 collective-permute-done.18.refs_9_
  83.9 3.8 %shard_map.80 = (f32[512,512]{1,0:T(8,128)S(1)}, f32[512,512]{1,0:T(8,128)S(1)}, f32[512,256]{1,0:T(8,128)S(1)}, f32[512,256]{1,0:T(8,128)S(1)}, bf16[1024,1792]...) custom-call(s32[4]{0:T(128)S(1)} %pad_add_fusion.numbers_ref, ...), custom_call_target="tpu_custom_call", output_to_operand_aliasing={{0}: (5, {}), {1}: (6, {}), {2}: (7, {}), {3}: (8, {})} | custom-call | flops 1431655808 | bytes 8388608 | tf_op jit(solution)/shard_map/pallas_call | solution.py:94
  87.8 0.0 collective-permute-done.13.refs_3_
  87.8 1.7 %shard_map.81 = (f32[512,512]{1,0:T(8,128)S(1)}, f32[512,512]{1,0:T(8,128)S(1)}, f32[512,256]{1,0:T(8,128)S(1)}, f32[512,256]{1,0:T(8,128)S(1)}) custom-call(s32[4]{0:T(128)S(1)} %pad_add_fusion.numbers_ref, bf16[512,512]{1,0:T(8,128)(2,1)S(1)} %collective-permute-done.2.refs_0_, ...), custom_call_target="tpu_custom_call", output_to_operand_aliasing={{0}: (5, {}), {1}: (6, {}), {2}: (7, {}), {3}: (8, {})} | custom-call | flops 1431655808 | bytes 8388608 | tf_op jit(solution)/shard_map/pallas_call | solution.py:94
  89.5 3.2 %shard_map.82 = (f32[512,512]{1,0:T(8,128)S(1)}, f32[512,512]{1,0:T(8,128)S(1)}, f32[512,256]{1,0:T(8,128)S(1)}, f32[512,256]{1,0:T(8,128)S(1)}) custom-call(s32[4]{0:T(128)S(1)} %pad_add_fusion.numbers_ref, bf16[512,512]{1,0:T(8,128)(2,1)S(1)} %collective-permute-done.2.refs_0_, ...), custom_call_target="tpu_custom_call", output_to_operand_aliasing={{0}: (5, {}), {1}: (6, {}), {2}: (7, {}), {3}: (8, {})} | custom-call | flops 1431655808 | bytes 8388608 | tf_op jit(solution)/shard_map/pallas_call | solution.py:94
  92.7 1.9 %shard_map.85 = (bf16[512,512]{1,0:T(8,128)(2,1)S(1)}, f32[512,512]{1,0:T(8,128)S(1)}, f32[512,256]{1,0:T(8,128)S(1)}) custom-call(s32[4]{0:T(128)S(1)} %pad_add_fusion.numbers_ref, bf16[512,512]{1,0:T(8,128)(2,1)S(1)} %collective-permute-done.7.refs_1_.refs_0_, ...), custom_call_target="tpu_custom_call", output_to_operand_aliasing={{1}: (4, {}), {2}: (5, {})} | custom-call | flops 715827904 | bytes 5242880 | tf_op jit(solution)/shard_map/pallas_call | solution.py:94
  94.6 4.1 %collective-permute-start.21 = (bf16[512,512]{1,0:T(8,128)(2,1)S(1)}, bf16[512,512]{1,0:T(8,128)(2,1)S(1)}, u32[]{:S(2)}, u32[]{:S(2)}) collective-permute-start(bf16[512,512]{1,0:T(8,128)(2,1)S(1)} %get-tuple-element.64), channel_id=1, source_target_pairs={{2,0},{4,1},{0,2},{6,3},{3,4},{5,5},{1,6},{7,7},{10,8},{12,9},{8,1... | collective-permute-start | bytes 1572872 | tf_op jit(solution)/shard_map/ppermute | solution.py:468
  98.7 1.5 %shard_map.83 = (f32[512,512]{1,0:T(8,128)S(1)}, f32[512,256]{1,0:T(8,128)S(1)}) custom-call(s32[4]{0:T(128)S(1)} %pad_add_fusion.numbers_ref, bf16[512,512]{1,0:T(8,128)(2,1)S(1)} %collective-permute-done.2.refs_0_, bf16[512,512]{1,0:T(8,128)(2,1)S(1)} %collective-permute-done.5.refs_1_, ...), custom_call_target="tpu_custom_call", output_to_operand_aliasing={{0}: (3, {}), {1}: (4, {})} | custom-call | flops 357913952 | bytes 4194304 | tf_op jit(solution)/shard_map/pallas_call | solution.py:94
  100.1 0.8 shard_map.84
  100.9 3.2 %collective-permute-start.19 = (bf16[512,512]{1,0:T(8,128)(2,1)S(1)}, bf16[512,512]{1,0:T(8,128)(2,1)S(1)}, u32[]{:S(2)}, u32[]{:S(2)}) collective-permute-start(bf16[512,512]{1,0:T(8,128)(2,1)S(1)} %get-tuple-element.61), channel_id=1, source_target_pairs={{0,0},{6,1},{2,2},{4,3},{1,4},{7,5},{3,6},{5,7},{8,8},{14,9},{10,1... | collective-permute-start | bytes 1572872 | tf_op jit(solution)/shard_map/ppermute | solution.py:468
  104.2 3.4 %collective-permute-done.21.refs_1_ = bf16[512,512]{1,0:T(8,128)(2,1)S(1)} collective-permute-done((bf16[512,512]{1,0:T(8,128)(2,1)S(1)}, bf16[512,512]{1,0:T(8,128)(2,1)S(1)}, u32[]{:S(2)}, u32[]{:S(2)}) %collective-permute-start.21) | collective-permute-done | bytes 524320 | tf_op jit(solution)/shard_map/ppermute | solution.py:468
  107.5 6.2 %collective-permute-start.22 = (bf16[512,512]{1,0:T(8,128)(2,1)S(1)}, bf16[512,512]{1,0:T(8,128)(2,1)S(1)}, u32[]{:S(2)}, u32[]{:S(2)}) collective-permute-start(bf16[512,512]{1,0:T(8,128)(2,1)S(1)} %collective-permute-done.21.refs_1_), channel_id=1, source_target_pairs={{0,1},{1,0},{2,3},{3,2},{4,5},{5,4},{6,7},{7,6},{8,9},{9,8},{10,11... | collective-permute-start | bytes 1572872 | tf_op jit(solution)/shard_map/ppermute | solution.py:449
  113.8 0.6 collective-permute-done.19.refs_0_
  114.4 2.6 %shard_map.86.refs_3_ = f32[512,1792]{1,0:T(8,128)S(1)} custom-call(s32[4]{0:T(128)S(1)} %pad_add_fusion.numbers_ref, bf16[512,512]{1,0:T(8,128)(2,1)S(1)} %collective-permute-done.19.refs_0_, bf16[512,512]{1,0:T(8,128)(2,1)S(1)} %collective-permute-done.21.refs_1_, bf16[1024,1792]{1,0:T(8,128)(2,1)S(1)} %get-tuple-element.66.refs_2_), custom_call_target="tpu_custom_call" | custom-call | flops 1879048192 | bytes 8388608 | tf_op jit(solution)/shard_map/pallas_call | solution.py:94
  117.0 0.0 copy-start.6
  117.1 3.2 %shard_map.87 = (f32[512,1792]{1,0:T(8,128)S(1)}, f32[512,128]{1,0:T(8,128)S(1)}) custom-call(s32[4]{0:T(128)S(1)} %pad_add_fusion.numbers_ref, bf16[512,512]{1,0:T(8,128)(2,1)S(1)} %collective-permute-done.20.refs_0_, bf16[512,512]{1,0:T(8,128)(2,1)S(1)} %collective-permute-done.22.refs_1_, ...), custom_call_target="tpu_custom_call", output_to_operand_aliasing={{0}: (4, {})} | custom-call | flops 1879048192 | bytes 12320768 | tf_op jit(solution)/shard_map/pallas_call | solution.py:94
  120.2 0.6 collective-permute-start.23
  120.8 1.2 collective-permute-done.23.refs_1_
  122.0 1.7 %shard_map.88 = bf16[512,1792]{1,0:T(8,128)(2,1)} custom-call(bf16[512,1792]{1,0:T(8,128)(2,1)S(1)} %copy-done.4, f32[512,1792]{1,0:T(8,128)S(1)} %get-tuple-element.67.share, f32[14,128]{1,0:T(8,128)S(1)} %bitcast.9, f32[512,128]{1,0:T(8,128)S(1)} %get-tuple-element.68.refs_0_, f32[512,128]{1,0:T(8,128)S(1)} %collective-permute-done.23.refs_1_), custom_call_target="tpu_custom_call" | custom-call | flops 7340032 | bytes 7340032 | tf_op jit(solution)/shard_map/pallas_call | solution.py:304
  (23 shorter events, 0.1 us)
Async XLA Ops:
  0.0 5.9 %collective-permute-start = (bf16[512,1792]{1,0:T(8,128)(2,1)}, bf16[512,1792]{1,0:T(8,128)(2,1)S(1)}, u32[]{:S(2)}, u32[]{:S(2)}) collective-permute-start(bf16[512,1792]{1,0:T(8,128)(2,1)} %tokens.1), channel_id=1, source_target_pairs={{0,1},{1,0},{2,3},{3,2},{4,5},{5,4},{6,7},{7,6},{8,9},{9,8},{10,11... | collective-permute-start | bytes 5505032 | tf_op jit(solution)/shard_map/ppermute | solution.py:449
  1.8 1.5 %copy-start.3 = (bf16[512,1792]{1,0:T(8,128)(2,1)S(1)}, bf16[512,1792]{1,0:T(8,128)(2,1)}, u32[]{:S(2)}) copy-start(bf16[512,1792]{1,0:T(8,128)(2,1)} %tokens.1) | copy-start | bytes 5505028
  3.3 2.6 %copy-start.1 = (bf16[3584,512]{1,0:T(8,128)(2,1)S(1)}, bf16[3584,512]{1,0:T(8,128)(2,1)}, u32[]{:S(2)}) copy-start(bf16[3584,512]{1,0:T(8,128)(2,1)} %refs_3_.4) | copy-start | bytes 11010052
  3.3 3.2 %copy-start.2 = (bf16[3584,512]{1,0:T(8,128)(2,1)S(1)}, bf16[3584,512]{1,0:T(8,128)(2,1)}, u32[]{:S(2)}) copy-start(bf16[3584,512]{1,0:T(8,128)(2,1)} %refs_4_.1) | copy-start | bytes 11010052
  3.3 3.7 %copy-start.4 = (bf16[512,1792]{1,0:T(8,128)(2,1)S(1)}, bf16[512,1792]{1,0:T(8,128)(2,1)}, u32[]{:S(2)}) copy-start(bf16[512,1792]{1,0:T(8,128)(2,1)} %tokens.1) | copy-start | bytes 5505028
  3.3 3.7 %copy-start.5 = (f32[3584]{0:T(1024)S(1)}, f32[3584]{0:T(1024)}, u32[]{:S(2)}) copy-start(f32[3584]{0:T(1024)} %param.8) | copy-start | bytes 43012
  4.3 1.6 %collective-permute-start.1 = (f32[512,128]{1,0:T(8,128)S(1)}, f32[512,128]{1,0:T(8,128)S(1)}, u32[]{:S(2)}, u32[]{:S(2)}) collective-permute-start(f32[512,128]{1,0:T(8,128)S(1)} %shard_map.73.refs_2_), channel_id=1, source_target_pairs={{0,1},{1,0},{2,3},{3,2},{4,5},{5,4},{6,7},{7,6},{8,9},{9,8},{10,11... | collective-permute-start | bytes 786440 | tf_op jit(solution)/shard_map/ppermute | solution.py:449
  6.9 4.1 %copy-start = (bf16[1024,3584]{1,0:T(8,128)(2,1)S(1)}, bf16[1024,3584]{1,0:T(8,128)(2,1)}, u32[]{:S(2)}) copy-start(bf16[1024,3584]{1,0:T(8,128)(2,1)} %refs_8_.3) | copy-start | bytes 22020100
  11.0 3.0 %slice-start = ((s8[7340032]{0:T(1024)(128)(4,1)}), s8[4194304]{0:T(1024)(128)(4,1)S(1)}, s32[]{:S(2)}) async-start(s8[7340032]{0:T(1024)(128)(4,1)} %bitcast.6), calls=%async_computation | async-start | bytes 8388608
  11.0 3.2 %slice-start.1 = ((s8[7340032]{0:T(1024)(128)(4,1)}), s8[3145728]{0:T(1024)(128)(4,1)S(1)}, s32[]{:S(2)}) async-start(s8[7340032]{0:T(1024)(128)(4,1)} %bitcast.6), calls=%async_computation.1 | async-start | bytes 6291456
  13.9 70.0 %collective-permute-start.18 = (bf16[1024,1792]{1,0:T(8,128)(2,1)S(1)}, bf16[1024,1792]{1,0:T(8,128)(2,1)S(1)}, u32[]{:S(2)}, u32[]{:S(2)}) collective-permute-start(bf16[1024,1792]{1,0:T(8,128)(2,1)S(1)} %get-tuple-element.48), channel_id=1, source_target_pairs={{0,1},{1,0},{2,3},{3,2},{4,5},{5,4},{6,7},{7,6},{8,9},{9,8},{10,11... | collective-permute-start | bytes 11010056 | tf_op jit(solution)/shard_map/ppermute | solution.py:449
  16.8 14.5 %collective-permute-start.7 = (bf16[512,512]{1,0:T(8,128)(2,1)S(1)}, bf16[512,512]{1,0:T(8,128)(2,1)S(1)}, u32[]{:S(2)}, u32[]{:S(2)}) collective-permute-start(bf16[512,512]{1,0:T(8,128)(2,1)S(1)} %shard_map.77), channel_id=1, source_target_pairs={{0,2},{1,4},{2,0},{3,6},{4,3},{5,5},{6,1},{7,7},{8,10},{9,12},{10,... | collective-permute-start | bytes 1572872 | tf_op jit(solution)/shard_map/ppermute | solution.py:465
  20.2 15.0 %collective-permute-start.10 = (bf16[512,512]{1,0:T(8,128)(2,1)S(1)}, bf16[512,512]{1,0:T(8,128)(2,1)S(1)}, u32[]{:S(2)}, u32[]{:S(2)}) collective-permute-start(bf16[512,512]{1,0:T(8,128)(2,1)S(1)} %get-tuple-element.39), channel_id=1, source_target_pairs={{0,8},{2,10},{4,12},{6,14},{8,16},{10,18},{12,20},{14,22},{16,24},... | collective-permute-start | bytes 1572872 | tf_op jit(solution)/shard_map/ppermute | solution.py:452
  23.4 16.6 %collective-permute-start.16 = (bf16[512,512]{1,0:T(8,128)(2,1)S(1)}, bf16[512,512]{1,0:T(8,128)(2,1)S(1)}, u32[]{:S(2)}, u32[]{:S(2)}) collective-permute-start(bf16[512,512]{1,0:T(8,128)(2,1)S(1)} %get-tuple-element.39), channel_id=1, source_target_pairs={{0,0},{1,6},{2,2},{3,4},{4,1},{5,7},{6,3},{7,5},{8,8},{9,14},{10,1... | collective-permute-start | bytes 1572872 | tf_op jit(solution)/shard_map/ppermute | solution.py:465
  26.8 19.6 %collective-permute-start.3 = (bf16[512,512]{1,0:T(8,128)(2,1)S(1)}, bf16[512,512]{1,0:T(8,128)(2,1)S(1)}, u32[]{:S(2)}, u32[]{:S(2)}) collective-permute-start(bf16[512,512]{1,0:T(8,128)(2,1)S(1)} %get-tuple-element.38), channel_id=1, source_target_pairs={{0,8},{2,10},{4,12},{6,14},{8,16},{10,18},{12,20},{14,22},{16,24},... | collective-permute-start | bytes 1572872 | tf_op jit(solution)/shard_map/ppermute | solution.py:452
  31.3 17.0 %collective-permute-start.2 = (bf16[512,512]{1,0:T(8,128)(2,1)S(1)}, bf16[512,512]{1,0:T(8,128)(2,1)S(1)}, u32[]{:S(2)}, u32[]{:S(2)}) collective-permute-start(bf16[512,512]{1,0:T(8,128)(2,1)S(1)} %shard_map.75), channel_id=1, source_target_pairs={{0,0},{1,6},{2,2},{3,4},{4,1},{5,7},{6,3},{7,5},{8,8},{9,14},{10,1... | collective-permute-start | bytes 1572872 | tf_op jit(solution)/shard_map/ppermute | solution.py:465
  35.2 23.8 %collective-permute-start.11 = (bf16[512,512]{1,0:T(8,128)(2,1)S(1)}, bf16[512,512]{1,0:T(8,128)(2,1)S(1)}, u32[]{:S(2)}, u32[]{:S(2)}) collective-permute-start(bf16[512,512]{1,0:T(8,128)(2,1)S(1)} %collective-permute-done.10), channel_id=1, source_target_pairs={{0,0},{1,6},{2,2},{3,4},{4,1},{5,7},{6,3},{7,5},{8,8},{9,14},{10,1... | collective-permute-start | bytes 1572872 | tf_op jit(solution)/shard_map/ppermute | solution.py:465
  40.0 23.2 %collective-permute-start.8 = (bf16[512,512]{1,0:T(8,128)(2,1)S(1)}, bf16[512,512]{1,0:T(8,128)(2,1)S(1)}, u32[]{:S(2)}, u32[]{:S(2)}) collective-permute-start(bf16[512,512]{1,0:T(8,128)(2,1)S(1)} %get-tuple-element.38), channel_id=1, source_target_pairs={{0,2},{1,4},{2,0},{3,6},{4,3},{5,5},{6,1},{7,7},{8,10},{9,12},{10,... | collective-permute-start | bytes 1572872 | tf_op jit(solution)/shard_map/ppermute | solution.py:465
  46.4 16.9 %collective-permute-start.4 = (bf16[512,512]{1,0:T(8,128)(2,1)S(1)}, bf16[512,512]{1,0:T(8,128)(2,1)S(1)}, u32[]{:S(2)}, u32[]{:S(2)}) collective-permute-start(bf16[512,512]{1,0:T(8,128)(2,1)S(1)} %collective-permute-done.3), channel_id=1, source_target_pairs={{0,2},{1,4},{2,0},{3,6},{4,3},{5,5},{6,1},{7,7},{8,10},{9,12},{10,... | collective-permute-start | bytes 1572872 | tf_op jit(solution)/shard_map/ppermute | solution.py:465
  48.3 16.9 %collective-permute-start.17 = (bf16[512,512]{1,0:T(8,128)(2,1)S(1)}, bf16[512,512]{1,0:T(8,128)(2,1)S(1)}, u32[]{:S(2)}, u32[]{:S(2)}) collective-permute-start(bf16[512,512]{1,0:T(8,128)(2,1)S(1)} %collective-permute-done.16.refs_2_), channel_id=1, source_target_pairs={{0,1},{1,0},{2,3},{3,2},{4,5},{5,4},{6,7},{7,6},{8,9},{9,8},{10,11... | collective-permute-start | bytes 1572872 | tf_op jit(solution)/shard_map/ppermute | solution.py:449
  59.0 13.2 %collective-permute-start.12 = (bf16[512,512]{1,0:T(8,128)(2,1)S(1)}, bf16[512,512]{1,0:T(8,128)(2,1)S(1)}, u32[]{:S(2)}, u32[]{:S(2)}) collective-permute-start(bf16[512,512]{1,0:T(8,128)(2,1)S(1)} %collective-permute-done.11.refs_2_), channel_id=1, source_target_pairs={{0,8},{2,10},{4,12},{6,14},{8,16},{10,18},{12,20},{14,22},{16,24},... | collective-permute-start | bytes 1572872 | tf_op jit(solution)/shard_map/ppermute | solution.py:452
  63.2 9.0 %collective-permute-start.15 = (bf16[512,512]{1,0:T(8,128)(2,1)S(1)}, bf16[512,512]{1,0:T(8,128)(2,1)S(1)}, u32[]{:S(2)}, u32[]{:S(2)}) collective-permute-start(bf16[512,512]{1,0:T(8,128)(2,1)S(1)} %collective-permute-done.11.refs_2_), channel_id=1, source_target_pairs={{0,1},{1,0},{2,3},{3,2},{4,5},{5,4},{6,7},{7,6},{8,9},{9,8},{10,11... | collective-permute-start | bytes 1572872 | tf_op jit(solution)/shard_map/ppermute | solution.py:449
  63.3 17.2 %collective-permute-start.5 = (bf16[512,512]{1,0:T(8,128)(2,1)S(1)}, bf16[512,512]{1,0:T(8,128)(2,1)S(1)}, u32[]{:S(2)}, u32[]{:S(2)}) collective-permute-start(bf16[512,512]{1,0:T(8,128)(2,1)S(1)} %collective-permute-done.4.refs_2_), channel_id=1, source_target_pairs={{0,8},{2,10},{4,12},{6,14},{8,16},{10,18},{12,20},{14,22},{16,24},... | collective-permute-start | bytes 1572872 | tf_op jit(solution)/shard_map/ppermute | solution.py:452
  65.2 18.7 %collective-permute-start.14 = (bf16[512,512]{1,0:T(8,128)(2,1)S(1)}, bf16[512,512]{1,0:T(8,128)(2,1)S(1)}, u32[]{:S(2)}, u32[]{:S(2)}) collective-permute-start(bf16[512,512]{1,0:T(8,128)(2,1)S(1)} %collective-permute-done.4.refs_2_), channel_id=1, source_target_pairs={{0,1},{1,0},{2,3},{3,2},{4,5},{5,4},{6,7},{7,6},{8,9},{9,8},{10,11... | collective-permute-start | bytes 1572872 | tf_op jit(solution)/shard_map/ppermute | solution.py:449
  72.2 15.6 %collective-permute-start.13 = (bf16[512,512]{1,0:T(8,128)(2,1)S(1)}, bf16[512,512]{1,0:T(8,128)(2,1)S(1)}, u32[]{:S(2)}, u32[]{:S(2)}) collective-permute-start(bf16[512,512]{1,0:T(8,128)(2,1)S(1)} %collective-permute-done.12.refs_2_), channel_id=1, source_target_pairs={{0,1},{1,0},{2,3},{3,2},{4,5},{5,4},{6,7},{7,6},{8,9},{9,8},{10,11... | collective-permute-start | bytes 1572872 | tf_op jit(solution)/shard_map/ppermute | solution.py:449
  72.2 17.3 %collective-permute-start.9 = (bf16[512,512]{1,0:T(8,128)(2,1)S(1)}, bf16[512,512]{1,0:T(8,128)(2,1)S(1)}, u32[]{:S(2)}, u32[]{:S(2)}) collective-permute-start(bf16[512,512]{1,0:T(8,128)(2,1)S(1)} %collective-permute-done.8.refs_2_), channel_id=1, source_target_pairs={{0,1},{1,0},{2,3},{3,2},{4,5},{5,4},{6,7},{7,6},{8,9},{9,8},{10,11... | collective-permute-start | bytes 1572872 | tf_op jit(solution)/shard_map/ppermute | solution.py:449
  80.5 12.2 %collective-permute-start.6 = (bf16[512,512]{1,0:T(8,128)(2,1)S(1)}, bf16[512,512]{1,0:T(8,128)(2,1)S(1)}, u32[]{:S(2)}, u32[]{:S(2)}) collective-permute-start(bf16[512,512]{1,0:T(8,128)(2,1)S(1)} %collective-permute-done.5.refs_1_), channel_id=1, source_target_pairs={{0,1},{1,0},{2,3},{3,2},{4,5},{5,4},{6,7},{7,6},{8,9},{9,8},{10,11... | collective-permute-start | bytes 1572872 | tf_op jit(solution)/shard_map/ppermute | solution.py:449
  94.6 13.0 %collective-permute-start.21 = (bf16[512,512]{1,0:T(8,128)(2,1)S(1)}, bf16[512,512]{1,0:T(8,128)(2,1)S(1)}, u32[]{:S(2)}, u32[]{:S(2)}) collective-permute-start(bf16[512,512]{1,0:T(8,128)(2,1)S(1)} %get-tuple-element.64), channel_id=1, source_target_pairs={{2,0},{4,1},{0,2},{6,3},{3,4},{5,5},{1,6},{7,7},{10,8},{12,9},{8,1... | collective-permute-start | bytes 1572872 | tf_op jit(solution)/shard_map/ppermute | solution.py:468
  100.9 13.5 %collective-permute-start.19 = (bf16[512,512]{1,0:T(8,128)(2,1)S(1)}, bf16[512,512]{1,0:T(8,128)(2,1)S(1)}, u32[]{:S(2)}, u32[]{:S(2)}) collective-permute-start(bf16[512,512]{1,0:T(8,128)(2,1)S(1)} %get-tuple-element.61), channel_id=1, source_target_pairs={{0,0},{6,1},{2,2},{4,3},{1,4},{7,5},{3,6},{5,7},{8,8},{14,9},{10,1... | collective-permute-start | bytes 1572872 | tf_op jit(solution)/shard_map/ppermute | solution.py:468
  107.5 9.5 %collective-permute-start.22 = (bf16[512,512]{1,0:T(8,128)(2,1)S(1)}, bf16[512,512]{1,0:T(8,128)(2,1)S(1)}, u32[]{:S(2)}, u32[]{:S(2)}) collective-permute-start(bf16[512,512]{1,0:T(8,128)(2,1)S(1)} %collective-permute-done.21.refs_1_), channel_id=1, source_target_pairs={{0,1},{1,0},{2,3},{3,2},{4,5},{5,4},{6,7},{7,6},{8,9},{9,8},{10,11... | collective-permute-start | bytes 1572872 | tf_op jit(solution)/shard_map/ppermute | solution.py:449
  114.4 2.6 %collective-permute-start.20 = (bf16[512,512]{1,0:T(8,128)(2,1)S(1)}, bf16[512,512]{1,0:T(8,128)(2,1)S(1)}, u32[]{:S(2)}, u32[]{:S(2)}) collective-permute-start(bf16[512,512]{1,0:T(8,128)(2,1)S(1)} %collective-permute-done.19.refs_0_), channel_id=1, source_target_pairs={{0,1},{1,0},{2,3},{3,2},{4,5},{5,4},{6,7},{7,6},{8,9},{9,8},{10,11... | collective-permute-start | bytes 1572872 | tf_op jit(solution)/shard_map/ppermute | solution.py:449
  117.0 4.9 %copy-start.6 = (f32[1792]{0:T(1024)S(1)}, f32[1792]{0:T(1024)}, u32[]{:S(2)}) copy-start(f32[1792]{0:T(1024)} %param.13) | copy-start | bytes 21508
  120.2 1.7 %collective-permute-start.23 = (f32[512,128]{1,0:T(8,128)S(1)}, f32[512,128]{1,0:T(8,128)S(1)}, u32[]{:S(2)}, u32[]{:S(2)}) collective-permute-start(f32[512,128]{1,0:T(8,128)S(1)} %get-tuple-element.68.refs_0_), channel_id=1, source_target_pairs={{0,1},{1,0},{2,3},{3,2},{4,5},{5,4},{6,7},{7,6},{8,9},{9,8},{10,11... | collective-permute-start | bytes 786440 | tf_op jit(solution)/shard_map/ppermute | solution.py:449
